TPU v7x, 32 devices: a 4x4x1 block of a 4x4x8 slice. The times are simulated.
32 devices in a mesh: rep: 1 (over z), kv: 32 (over y, x, core).
Axes of the slice: x: 4, y: 4, z: 1, core: 2. Of those that a mesh axis runs over, the one named last changes fastest.
The devices are a block of a 4x4x8 slice.
Arguments:
- embeds: bfloat16 [2, 128, 2048], P(None, ('rep', 'kv'))
- w_query: bfloat16 [2, 2048, 2048], replicated
- w_key: bfloat16 [2, 2048, 2048], replicated
- w_value: bfloat16 [2, 2048, 2048], replicated
- w_out: bfloat16 [2, 2048, 2048], replicated
- w_up: bfloat16 [2, 2048, 8192], replicated
- w_down: bfloat16 [2, 8192, 2048], replicated
- k_pool: bfloat16 [2304, 2, 16, 16, 128], P(('rep', 'kv'))
- v_pool: bfloat16 [2304, 2, 16, 16, 128], P(('rep', 'kv'))
- old_table: int32 [128, 12], P('rep')
- new_table: int32 [128, 12], P('rep')
- seq_len: int32 [128], P('rep')
- finished: int32 [128], P('rep')
- mig_src: int32 [768], P('rep')
- mig_dst: int32 [768], P('rep')
Outputs:
- output 1: bfloat16 [2, 128, 2048], P(None, ('rep', 'kv'))
- output 2: bfloat16 [2304, 2, 16, 16, 128], P(('rep', 'kv'))
- output 3: bfloat16 [2304, 2, 16, 16, 128], P(('rep', 'kv'))
All inputs are finite; a program needn't handle non-finite values.
Results may differ from a plain program's by a relative error of at most 0.0188525.
Values are sent between devices in bfloat16 or wider.
A program may use at most 768 MiB of HBM per device.

v0:
```python
import functools

import jax
import jax.numpy as jnp
from jax import lax
from jax.experimental import pallas as pl
from jax.experimental.pallas import tpu as pltpu
from jax.sharding import PartitionSpec as P

MESH = pl.DeviceIdType.MESH
ANY = pl.BlockSpec(memory_space=pl.ANY)
VMEM = pl.BlockSpec(memory_space=pltpu.VMEM)
SMEM = pl.BlockSpec(memory_space=pltpu.SMEM)
LOW = -1e30


def ring(count, depth, lead, start_in, wait_in, start_out, wait_out):
    def body(i, carry):
        @pl.when(i < count)
        def _():
            @pl.when(i >= depth)
            def _():
                wait_out(i - depth)

            start_in(i)

        @pl.when(i >= lead)
        def _():
            wait_in(i - lead)
            start_out(i - lead)

        return carry

    lax.fori_loop(0, count + lead, body, 0)

    def drain(i, carry):
        wait_out(i)
        return carry

    lax.fori_loop(jnp.maximum(count - depth, 0), count, drain, 0)


def compact(total, flag, value, listed):
    def body(i, count):
        @pl.when(flag(i))
        def _():
            listed[count] = value(i)

        return count + flag(i).astype(jnp.int32)

    return lax.fori_loop(0, total, body, jnp.int32(0))


def pack_kernel(depth, lead, plan, slot_ref, *rest):
    pools = rest[:2]
    outs = rest[2:-4]
    buf, listed, sems_in, sems_out = rest[-4:]
    peers = outs[0].shape[0]
    for r, halves in plan:
        mine, outs = outs[0], outs[1:]
        count = compact(peers, lambda i: slot_ref[r * peers + i] >= 0, lambda i: i, listed)

        def ins(i):
            at = lax.rem(i, depth)
            slot = slot_ref[r * peers + listed[i]]
            return [pltpu.make_async_copy(pools[h].at[slot], buf.at[at, h], sems_in.at[at, h]) for h in halves]

        def puts(i):
            at = lax.rem(i, depth)
            return [pltpu.make_async_copy(buf.at[at, h], mine.at[listed[i], k], sems_out.at[at, h]) for k, h in enumerate(halves)]

        ring(
            count, depth, lead,
            lambda i: [c.start() for c in ins(i)],
            lambda i: [c.wait() for c in ins(i)],
            lambda i: [c.start() for c in puts(i)],
            lambda i: [c.wait() for c in puts(i)],
        )


def pack_pages(plan, send_slot, k_pool, v_pool, peers):
    page = k_pool.shape[1:]
    depth, lead = 24, 12
    total = sum(len(halves) for _, halves in plan)
    return pl.pallas_call(
        functools.partial(pack_kernel, depth, lead, plan),
        out_shape=[jax.ShapeDtypeStruct((peers, len(halves)) + page, k_pool.dtype) for _, halves in plan],
        in_specs=[SMEM, ANY, ANY],
        out_specs=[ANY] * len(plan),
        scratch_shapes=[
            pltpu.VMEM((depth, 2) + page, k_pool.dtype),
            pltpu.SMEM((peers,), jnp.int32),
            pltpu.SemaphoreType.DMA((depth, 2)),
            pltpu.SemaphoreType.DMA((depth, 2)),
        ],
        cost_estimate=pl.CostEstimate(flops=10 ** 8 * total, bytes_accessed=2 ** 21 * total, transcendentals=0),
        name="pack_pages",
    )(send_slot, k_pool, v_pool)


def keep_kernel(depth, lead, from_ref, k_ref, v_ref, k_out, v_out, buf, listed, sems_in, sems_out):
    count = compact(from_ref.shape[0], lambda i: from_ref[i] < 0, lambda i: i, listed)

    def ins(i):
        at = lax.rem(i, depth)
        return [pltpu.make_async_copy(ref.at[listed[i]], buf.at[at, h], sems_in.at[at, h]) for h, ref in enumerate((k_ref, v_ref))]

    def outs(i):
        at = lax.rem(i, depth)
        return [pltpu.make_async_copy(buf.at[at, h], ref.at[listed[i]], sems_out.at[at, h]) for h, ref in enumerate((k_out, v_out))]

    ring(
        count, depth, lead,
        lambda i: [c.start() for c in ins(i)],
        lambda i: [c.wait() for c in ins(i)],
        lambda i: [c.start() for c in outs(i)],
        lambda i: [c.wait() for c in outs(i)],
    )


def keep_pages(from_page, k_pool, v_pool):
    depth, lead = 24, 12
    return pl.pallas_call(
        functools.partial(keep_kernel, depth, lead),
        out_shape=[jax.ShapeDtypeStruct(k_pool.shape, k_pool.dtype)] * 2,
        in_specs=[SMEM] + [ANY] * 2,
        out_specs=[ANY] * 2,
        scratch_shapes=[
            pltpu.VMEM((depth, 2) + k_pool.shape[1:], k_pool.dtype),
            pltpu.SMEM((k_pool.shape[0],), jnp.int32),
            pltpu.SemaphoreType.DMA((depth, 2)),
            pltpu.SemaphoreType.DMA((depth, 2)),
        ],
        cost_estimate=pl.CostEstimate(flops=10 ** 9, bytes_accessed=2 ** 25, transcendentals=0),
        name="keep_pages",
    )(from_page, k_pool, v_pool)


def place_kernel(depth, lead, plan, patches, seq_dev, n_rows, from_ref, first_ref, second_ref, offset_ref, *rest):
    arrived, rest = rest[:len(plan)], rest[len(plan):]
    rows = rest[:n_rows]
    k_out, v_out, buf, listed, sems_in, sems_out, staged, entries, sem_row = rest[n_rows + 2:]
    pools = (k_out, v_out)
    peers = arrived[0].shape[0]
    slots, n_batch = from_ref.shape[0], offset_ref.shape[0]
    heads = k_out.shape[3]

    def came(slot, r):
        return (from_ref[slot] >= r * peers) & (from_ref[slot] < (r + 1) * peers)

    def fetch(at, seq, step, h):
        home, place = seq // seq_dev, lax.rem(seq, seq_dev)
        return [
            pltpu.make_async_copy(
                x.at[lax.rem(home, 2), home // 2, 1 + h, place, pl.ds(step * heads, heads)], staged.at[at, layer], sem_row.at[0]
            )
            for layer, x in enumerate(rows)
        ]

    ends = []
    found = jnp.int32(0)
    for h, rounds, inside in patches:
        def collect(slot, count):
            hit = jnp.bool_(False)
            for r in rounds:
                hit = hit | came(slot, r)
            for step, ref in enumerate((first_ref, second_ref)):
                seq = ref[slot]
                take = (seq >= 0) & (hit == inside)

                @pl.when(take)
                def _():
                    entries[count] = (slot * 2 + step) * n_batch + seq
                    for c in fetch(count, seq, step, h):
                        c.start()

                count = count + take.astype(jnp.int32)
            return count

        found = lax.fori_loop(0, slots, collect, found)
        ends.append(found)

    for part, (r, halves) in enumerate(plan):
        count = compact(slots, lambda i: came(i, r), lambda i: i, listed)

        def ins(i):
            at = lax.rem(i, depth)
            line = from_ref[listed[i]] - r * peers
            return [pltpu.make_async_copy(arrived[part].at[line, k], buf.at[at, h], sems_in.at[at, h]) for k, h in enumerate(halves)]

        def outs(i):
            at = lax.rem(i, depth)
            return [pltpu.make_async_copy(buf.at[at, h], pools[h].at[listed[i]], sems_out.at[at, h]) for h in halves]

        ring(
            count, depth, lead,
            lambda i: [c.start() for c in ins(i)],
            lambda i: [c.wait() for c in ins(i)],
            lambda i: [c.start() for c in outs(i)],
            lambda i: [c.wait() for c in outs(i)],
        )

    if patches:
        def fetched(i, carry):
            for c in fetch(i, 0, 0, 0):
                c.wait()
            return carry

        lax.fori_loop(0, found, fetched, 0)
        begin = jnp.int32(0)
        for (h, _, _), end in zip(patches, ends):
            def row_outs(i):
                entry = entries[i]
                seq, at = lax.rem(entry, n_batch), entry // n_batch
                slot, step = at // 2, lax.rem(at, 2)
                return [
                    pltpu.make_async_copy(staged.at[i, layer], pools[h].at[slot, layer, offset_ref[seq] + step], sem_row.at[1])
                    for layer in range(n_rows)
                ]

            def start(i, carry):
                for c in row_outs(i):
                    c.start()
                return carry

            lax.fori_loop(begin, end, start, 0)
            begin = end

        def written(i, carry):
            for layer in range(n_rows):
                pltpu.make_async_copy(staged.at[i, layer], k_out.at[0, layer, 0], sem_row.at[1]).wait()
            return carry

        lax.fori_loop(0, found, written, 0)


def place_pages(plan, patches, seq_dev, from_page, first_seq, second_seq, offsets, arrived, rows, k_out, v_out):
    depth, lead = 24, 12
    first_pool = 4 + len(arrived) + len(rows)
    most = max(2 * len(patches) * k_out.shape[0], 1)
    return pl.pallas_call(
        functools.partial(place_kernel, depth, lead, plan, patches, seq_dev, len(rows)),
        out_shape=[jax.ShapeDtypeStruct(k_out.shape, k_out.dtype)] * 2,
        in_specs=[SMEM] * 4 + [ANY] * (len(arrived) + len(rows) + 2),
        out_specs=[ANY] * 2,
        scratch_shapes=[
            pltpu.VMEM((depth, 2) + k_out.shape[1:], k_out.dtype),
            pltpu.SMEM((k_out.shape[0],), jnp.int32),
            pltpu.SemaphoreType.DMA((depth, 2)),
            pltpu.SemaphoreType.DMA((depth, 2)),
            pltpu.VMEM((most, max(len(rows), 1)) + k_out.shape[3:], k_out.dtype),
            pltpu.SMEM((most,), jnp.int32),
            pltpu.SemaphoreType.DMA((2,)),
        ],
        input_output_aliases={first_pool: 0, first_pool + 1: 1},
        cost_estimate=pl.CostEstimate(flops=2 * 10 ** 8 * len(arrived), bytes_accessed=2 ** 22 * len(arrived), transcendentals=0),
        name="place_pages",
    )(from_page, first_seq, second_seq, offsets, *arrived, *rows, k_out, v_out)


def attend_kernel(block, pages_seq, seq_dev, page_size, scale, code_ref, x_ref, k_ref, v_ref, acc_ref):
    rows, head_dim = x_ref.shape[-2:]
    heads = k_ref.shape[3]
    chips = acc_ref.shape[1]
    step = pl.program_id(0)

    @pl.when(step == 0)
    def _():
        for core in range(2):
            acc_ref[core, :, :seq_dev] = jnp.zeros((chips, seq_dev, rows, head_dim), jnp.float32)
            lane = lax.broadcasted_iota(jnp.int32, (chips, 1, rows, head_dim), 3)
            acc_ref[core, :, seq_dev:] = jnp.where(lax.rem(lane, 2) == 0, LOW, 0.0)

    row = lax.broadcasted_iota(jnp.int32, (rows, page_size * heads), 0)
    column = lax.broadcasted_iota(jnp.int32, (rows, page_size * heads), 1)
    same_head = lax.rem(row, heads) == lax.rem(column, heads)
    position = jnp.where(same_head, column // heads, page_size)
    lane = lax.broadcasted_iota(jnp.int32, (rows, head_dim), 1)
    found = []
    for s in range(block):
        code = code_ref[step * block + s]
        held = jnp.maximum(code, 0)
        seen = jnp.where(code >= 0, lax.rem(held, 2 * page_size), 0)
        seq = held // (2 * page_size * pages_seq)
        home, place = seq // seq_dev, lax.rem(seq, seq_dev)
        core, chip = lax.rem(home, 2), home // 2
        q = x_ref[core, chip, 0, place]
        keys = k_ref[s, 0].reshape(page_size * heads, head_dim)
        values = v_ref[s, 0].reshape(page_size * heads, head_dim)
        scores = lax.dot_general(q, keys, (((1,), (1,)), ((), ())), preferred_element_type=jnp.float32) * scale
        mask = position < seen
        scores = jnp.where(mask, scores, LOW)
        top = jnp.max(scores, axis=1, keepdims=True)
        weights = jnp.where(mask, jnp.exp(scores - top), 0.0)
        total = jnp.sum(weights, axis=1, keepdims=True)
        high = weights.astype(jnp.bfloat16)
        low = (weights - high.astype(jnp.float32)).astype(jnp.bfloat16)
        mixed = jnp.dot(high, values, preferred_element_type=jnp.float32) + jnp.dot(low, values, preferred_element_type=jnp.float32)
        found.append((core, chip, place, top, total, mixed))
    for core, chip, place, top, total, mixed in found:
        stats = acc_ref[core, chip, seq_dev]
        old_top = jnp.max(jnp.where(lane == 2 * place, stats, LOW), axis=1, keepdims=True)
        old_total = jnp.sum(jnp.where(lane == 2 * place + 1, stats, 0.0), axis=1, keepdims=True)
        new_top = jnp.maximum(top, old_top)
        old_part, new_part = jnp.exp(old_top - new_top), jnp.exp(top - new_top)
        acc_ref[core, chip, place] = acc_ref[core, chip, place] * old_part + mixed * new_part
        new_total = old_total * old_part + total * new_part
        acc_ref[core, chip, seq_dev] = jnp.where(lane == 2 * place, new_top, jnp.where(lane == 2 * place + 1, new_total, stats))


def attend_pages(code, x_all, k_pool, v_pool, layer, pages_seq):
    slots, _, page_size, heads, head_dim = k_pool.shape
    cores, chips, _, seq_dev, rows, _ = x_all.shape
    block = 8
    page_spec = pl.BlockSpec((block, 1, page_size, heads, head_dim), lambda i, c: (i, layer, 0, 0, 0))
    query_spec = pl.BlockSpec((cores, chips, 1, seq_dev, rows, head_dim), lambda i, c: (0,) * 6)
    acc_shape = (cores, chips, seq_dev + 1, rows, head_dim)
    return pl.pallas_call(
        functools.partial(attend_kernel, block, pages_seq, seq_dev, page_size, head_dim ** -0.5),
        out_shape=jax.ShapeDtypeStruct(acc_shape, jnp.float32),
        grid_spec=pltpu.PrefetchScalarGridSpec(
            num_scalar_prefetch=1,
            grid=(slots // block,),
            in_specs=[query_spec, page_spec, page_spec],
            out_specs=pl.BlockSpec(acc_shape, lambda i, c: (0,) * 5),
        ),
        compiler_params=pltpu.CompilerParams(dimension_semantics=("arbitrary",)),
        cost_estimate=pl.CostEstimate(flops=10 ** 9, bytes_accessed=2 * slots * page_size * heads * head_dim * 2, transcendentals=0),
        name="attend_pages",
    )(code, x_all, k_pool, v_pool)


def spread_kernel(n, x_ref, out_ref, held, send_sem, recv_sem, pass_sem, got_sem, copy_sem):
    me = lax.axis_index("kv")
    chips = n // 2
    core, chip = lax.rem(me, 2), me // 2
    other = me + 1 - 2 * core

    def peer(j):
        return 2 * lax.rem(chip + j, chips) + core

    barrier = pltpu.get_barrier_semaphore()

    def greet(j, carry):
        pl.semaphore_signal(barrier, inc=1, device_id={"kv": peer(j)}, device_id_type=MESH)
        return carry

    lax.fori_loop(1, chips, greet, 0)
    pl.semaphore_signal(barrier, inc=1, device_id={"kv": other}, device_id_type=MESH)
    pl.semaphore_wait(barrier, chips)

    def send(j):
        return pltpu.make_async_remote_copy(
            src_ref=x_ref, dst_ref=held.at[core, chip], send_sem=send_sem.at[j], recv_sem=recv_sem.at[chip],
            device_id={"kv": peer(j)}, device_id_type=MESH,
        )

    def forward(source, at):
        return pltpu.make_async_remote_copy(
            src_ref=source, dst_ref=held.at[core, at], send_sem=pass_sem.at[at], recv_sem=got_sem.at[at],
            device_id={"kv": other}, device_id_type=MESH,
        )

    def start(j, carry):
        send(j).start()
        return carry

    lax.fori_loop(1, chips, start, 0)
    own = forward(x_ref, chip)
    own.start()
    mine = pltpu.make_async_copy(x_ref, out_ref.at[core, chip], copy_sem.at[0])
    mine.start()

    def arrive(j, carry):
        at = lax.rem(chip + chips - j, chips)
        pltpu.make_async_remote_copy(
            src_ref=x_ref, dst_ref=held.at[core, at], send_sem=send_sem.at[j], recv_sem=recv_sem.at[at],
            device_id={"kv": other}, device_id_type=MESH,
        ).wait_recv()
        forward(held.at[core, at], at).start()
        pltpu.make_async_copy(held.at[core, at], out_ref.at[core, at], copy_sem.at[j]).start()
        return carry

    lax.fori_loop(1, chips, arrive, 0)

    def passed(j, carry):
        at = lax.rem(chip + j, chips)
        pltpu.make_async_remote_copy(
            src_ref=x_ref, dst_ref=held.at[1 - core, at], send_sem=pass_sem.at[at], recv_sem=got_sem.at[at],
            device_id={"kv": other}, device_id_type=MESH,
        ).wait_recv()
        pltpu.make_async_copy(held.at[1 - core, at], out_ref.at[1 - core, at], copy_sem.at[chips + j]).start()
        return carry

    lax.fori_loop(0, chips, passed, 0)

    own.wait_send()
    mine.wait()

    def finish(j, carry):
        at = lax.rem(chip + chips - j, chips)
        send(j).wait_send()
        forward(held.at[core, at], at).wait_send()
        pltpu.make_async_copy(held.at[core, at], out_ref.at[core, at], copy_sem.at[j]).wait()
        return carry

    lax.fori_loop(1, chips, finish, 0)

    def written(j, carry):
        at = lax.rem(chip + j, chips)
        pltpu.make_async_copy(held.at[1 - core, at], out_ref.at[1 - core, at], copy_sem.at[chips + j]).wait()
        return carry

    lax.fori_loop(0, chips, written, 0)


def spread(x, n):
    chips = n // 2
    return pl.pallas_call(
        functools.partial(spread_kernel, n),
        out_shape=jax.ShapeDtypeStruct((2, chips) + x.shape, x.dtype),
        in_specs=[VMEM],
        out_specs=ANY,
        scratch_shapes=[
            pltpu.VMEM((2, chips) + x.shape, x.dtype),
            pltpu.SemaphoreType.DMA((chips,)),
            pltpu.SemaphoreType.DMA((chips,)),
            pltpu.SemaphoreType.DMA((chips,)),
            pltpu.SemaphoreType.DMA((chips,)),
            pltpu.SemaphoreType.DMA((n,)),
        ],
        compiler_params=pltpu.CompilerParams(collective_id=0, has_side_effects=True),
        name="spread_queries",
    )(x)


def lane_before(x):
    return pltpu.roll(x, x.shape[1] - 1, 1)


def merge_chip_kernel(acc_ref, sums_ref, near, send_sem, recv_sem):
    me = lax.axis_index("kv")
    core = lax.rem(me, 2)
    other = me + 1 - 2 * core
    chips, blocks, rows, head_dim = near.shape
    seq_dev = blocks - 1

    barrier = pltpu.get_barrier_semaphore()
    pl.semaphore_signal(barrier, inc=1, device_id={"kv": other}, device_id_type=MESH)
    pl.semaphore_wait(barrier, 1)

    swap = pltpu.make_async_remote_copy(
        src_ref=acc_ref.at[1 - core], dst_ref=near, send_sem=send_sem.at[0], recv_sem=recv_sem.at[0],
        device_id={"kv": other}, device_id_type=MESH,
    )
    swap.start()
    even = lax.rem(lax.broadcasted_iota(jnp.int32, (rows, head_dim), 1), 2) == 0
    swap.wait_recv()

    def merge(at, carry):
        mine, theirs = acc_ref[core, at, seq_dev], near[at, seq_dev]
        top = jnp.maximum(mine, theirs)
        a, b = jnp.exp(mine - top), jnp.exp(theirs - top)
        total = a * lane_before(mine) + b * lane_before(theirs)
        sums_ref[at, seq_dev] = jnp.where(even, top, pltpu.roll(total, 1, 1))
        for i in range(seq_dev):
            sums_ref[at, i] = a[:, 2 * i:2 * i + 1] * acc_ref[core, at, i] + b[:, 2 * i:2 * i + 1] * near[at, i]
        return carry

    lax.fori_loop(0, chips, merge, 0)
    swap.wait_send()


def merge_chip(acc):
    blocks = acc.shape[1:]
    return pl.pallas_call(
        merge_chip_kernel,
        out_shape=jax.ShapeDtypeStruct(blocks, acc.dtype),
        in_specs=[VMEM],
        out_specs=VMEM,
        scratch_shapes=[
            pltpu.VMEM(blocks, acc.dtype),
            pltpu.SemaphoreType.DMA((1,)),
            pltpu.SemaphoreType.DMA((1,)),
        ],
        compiler_params=pltpu.CompilerParams(collective_id=2, has_side_effects=True),
        cost_estimate=pl.CostEstimate(flops=10 ** 9, bytes_accessed=2 ** 23, transcendentals=0),
        name="merge_chip",
    )(acc)


def gather_home_kernel(n, scale, sums_ref, x_ref, o_ref, held, send_sem, recv_sem):
    me = lax.axis_index("kv")
    _, seq_dev, rows, head_dim = x_ref.shape
    heads = rows // 2
    chips = n // 2
    core, chip = lax.rem(me, 2), me // 2

    def peer(j):
        return 2 * lax.rem(chip + j, chips) + core

    barrier = pltpu.get_barrier_semaphore()

    def greet(j, carry):
        pl.semaphore_signal(barrier, inc=1, device_id={"kv": peer(j)}, device_id_type=MESH)
        return carry

    lax.fori_loop(1, chips, greet, 0)
    pl.semaphore_wait(barrier, chips - 1)

    def send(j):
        return pltpu.make_async_remote_copy(
            src_ref=sums_ref.at[lax.rem(chip + j, chips)], dst_ref=held.at[chip], send_sem=send_sem.at[j], recv_sem=recv_sem.at[chip],
            device_id={"kv": peer(j)}, device_id_type=MESH,
        )

    def start(j, carry):
        send(j).start()
        return carry

    lax.fori_loop(1, chips, start, 0)
    held[chip] = sums_ref[chip]

    queries = [x_ref[0, i].astype(jnp.float32) for i in range(seq_dev)]
    second_row = lax.broadcasted_iota(jnp.int32, (rows, 1), 0) >= heads

    def twice(h, i, step):
        x = x_ref[1 + h, i, step * heads:(step + 1) * heads].astype(jnp.float32)
        return jnp.concatenate([x, x], axis=0)

    first = [jnp.sum(queries[i] * twice(0, i, 0), axis=1, keepdims=True) * scale for i in range(seq_dev)]
    second = [
        jnp.where(second_row, jnp.sum(queries[i] * twice(0, i, 1), axis=1, keepdims=True) * scale, LOW)
        for i in range(seq_dev)
    ]
    def arrive(j, carry):
        at = lax.rem(chip + chips - j, chips)
        pltpu.make_async_remote_copy(
            src_ref=sums_ref.at[at], dst_ref=held.at[at], send_sem=send_sem.at[j], recv_sem=recv_sem.at[at],
            device_id={"kv": peer(j)}, device_id_type=MESH,
        ).wait_recv()
        return carry

    lax.fori_loop(1, chips, arrive, 0)

    def highest(j, top):
        return jnp.maximum(top, held[j, seq_dev])

    top_all = lax.fori_loop(0, chips, highest, jnp.full((rows, head_dim), LOW, jnp.float32))
    tops, totals, mixed = [], [], []
    for i in range(seq_dev):
        top = jnp.maximum(jnp.maximum(top_all[:, 2 * i:2 * i + 1], first[i]), second[i])
        p_first, p_second = jnp.exp(first[i] - top), jnp.exp(second[i] - top)
        tops.append(top)
        totals.append(p_first + p_second)
        mixed.append(p_first * twice(1, i, 0) + p_second * twice(1, i, 1))

    def merge(j, carry):
        totals, mixed = carry
        stats = held[j, seq_dev]
        new_totals, new_mixed = [], []
        for i in range(seq_dev):
            weight = jnp.exp(stats[:, 2 * i:2 * i + 1] - tops[i])
            new_totals.append(totals[i] + weight * stats[:, 2 * i + 1:2 * i + 2])
            new_mixed.append(mixed[i] + weight * held[j, i])
        return tuple(new_totals), tuple(new_mixed)

    totals, mixed = lax.fori_loop(0, chips, merge, (tuple(totals), tuple(mixed)))
    for i in range(seq_dev):
        o_ref[i] = (mixed[i] / totals[i]).astype(o_ref.dtype)

    def finish(j, carry):
        send(j).wait_send()
        return carry

    lax.fori_loop(1, chips, finish, 0)


def gather_home(sums, x, n):
    chips = n // 2
    return pl.pallas_call(
        functools.partial(gather_home_kernel, n, x.shape[-1] ** -0.5),
        out_shape=jax.ShapeDtypeStruct(x.shape[1:], jnp.bfloat16),
        in_specs=[VMEM] * 2,
        out_specs=VMEM,
        scratch_shapes=[
            pltpu.VMEM(sums.shape, sums.dtype),
            pltpu.SemaphoreType.DMA((chips,)),
            pltpu.SemaphoreType.DMA((chips,)),
        ],
        compiler_params=pltpu.CompilerParams(collective_id=1, has_side_effects=True),
        name="gather_home",
    )(sums, x)


def solution(mesh):
    groups = mesh.shape['kv']
    rows_spec = P(None, ('rep', 'kv'), None)
    pool_spec = P(('rep', 'kv'))
    table_spec = P('rep', None)
    vec_spec = P('rep')
    full_spec = P()

    def device_fn(embeds, w_query, w_key, w_value, w_out, w_up, w_down, k_pool, v_pool, old_table, new_table, seq_len, finished, mig_src, mig_dst):
        me = lax.axis_index('kv')
        slots, n_layers, page_size, heads, head_dim = k_pool.shape
        steps, seq_dev, width = embeds.shape
        n_batch, pages_seq = old_table.shape
        n_mig = mig_src.shape[0]
        rounds = 4 * n_mig // (groups * groups)
        base = me * slots
        local = jnp.arange(slots, dtype=jnp.int32)
        active = finished == 0
        last = pages_seq - 1

        def find(match, value):
            return jnp.max(jnp.where(match, value, -1), axis=1)

        flat = old_table.reshape(-1)
        place = jnp.arange(n_batch * pages_seq, dtype=jnp.int32)
        seen = jnp.clip(seq_len[:, None] - jnp.arange(pages_seq, dtype=jnp.int32)[None, :] * page_size, 0, page_size).reshape(-1)
        code = find(flat[None, :] - base == local[:, None], (place * (2 * page_size) + seen)[None, :])

        src_dev, dst_dev = mig_src // slots, mig_dst // slots
        pair = src_dev * groups + dst_dev
        entry = jnp.arange(n_mig, dtype=jnp.int32)
        rank = jnp.sum((pair[None, :] == pair[:, None]) & (entry[None, :] < entry[:, None]), axis=1, dtype=jnp.int32)
        lines = jnp.arange(rounds * groups, dtype=jnp.int32)
        send_slot = find(
            ((rank * groups + dst_dev)[None, :] == lines[:, None]) & (src_dev == me)[None, :], (mig_src - src_dev * slots)[None, :]
        )
        from_page = find((mig_dst - base)[None, :] == local[:, None], (rank * groups + src_dev)[None, :])

        seq_ids = jnp.arange(n_batch, dtype=jnp.int32)
        owner_old = find((old_table[:, last] - base)[None, :] == local[:, None], seq_ids[None, :])
        owner_new = find(((new_table[:, last] - base)[None, :] == local[:, None]) & active[None, :], seq_ids[None, :])
        first_seq = jnp.where(from_page >= 0, owner_new, owner_old)
        second_seq = owner_new
        offsets = lax.rem(seq_len, page_size)

        def exchange(block):
            return lax.all_to_all(block, 'kv', 0, 0, tiled=True)

        def send_next(value, count):
            for block in packed[len(got):len(got) + count]:
                block, value = lax.optimization_barrier((block, value))
                got.append(exchange(block))
            return value

        plan = ((0, (0,)), (0, (1,))) + tuple((r, (0, 1)) for r in range(1, rounds - 1)) + ((rounds - 1, (0,)), (rounds - 1, (1,)))
        packed = list(pack_pages(plan[:1], send_slot, k_pool, v_pool, groups))
        got = [exchange(packed[0])]
        packed += list(pack_pages(plan[1:], send_slot, k_pool, v_pool, groups))
        tables = (from_page, first_seq, second_seq, offsets)
        k_out, v_out = keep_pages(from_page, k_pool, v_pool)

        hidden = jnp.transpose(embeds, (1, 0, 2)).reshape(seq_dev * steps, width)
        rows = []
        for layer in range(n_layers):
            x = jnp.stack([
                jnp.dot(hidden, w[layer], preferred_element_type=jnp.float32).astype(jnp.bfloat16).reshape(seq_dev, steps * heads, head_dim)
                for w in (w_query, w_key, w_value)
            ])
            x, k_out, v_out, packed = lax.optimization_barrier((x, k_out, v_out, packed))
            x_all = spread(x, groups)
            rows.append(x_all)
            x_all = send_next(x_all, 1)
            acc = attend_pages(code, x_all, k_pool, v_pool, layer, pages_seq)
            mixed = gather_home(merge_chip(acc), x, groups)
            mixed = send_next(mixed, 1 if layer + 1 < n_layers else len(plan))
            if layer == 0:
                k_out, v_out = place_pages(plan[:2], (), seq_dev, *tables, got[:2], [], k_out, v_out)
            mixed = mixed.reshape(seq_dev * steps, heads * head_dim)
            hidden = (hidden.astype(jnp.float32) + jnp.dot(mixed, w_out[layer], preferred_element_type=jnp.float32)).astype(jnp.bfloat16)
            inner = jax.nn.gelu(jnp.dot(hidden, w_up[layer], preferred_element_type=jnp.float32)).astype(jnp.bfloat16)
            hidden = (hidden.astype(jnp.float32) + jnp.dot(inner, w_down[layer], preferred_element_type=jnp.float32)).astype(jnp.bfloat16)
        last_round = (rounds - 1,)
        k_out, v_out = place_pages(
            plan[2:-1], ((0, (), False), (1, last_round, False)), seq_dev, *tables, got[2:-1], rows, k_out, v_out
        )
        k_out, v_out = place_pages(plan[-1:], ((1, last_round, True),), seq_dev, *tables, got[-1:], rows, k_out, v_out)
        hidden = jnp.transpose(hidden.reshape(seq_dev, steps, width), (1, 0, 2))
        done = lax.dynamic_slice(finished, (me * seq_dev,), (seq_dev,)) != 0
        live = jnp.stack([jnp.ones_like(done), ~done])
        hidden = jnp.where(live[:, :, None], hidden, jnp.zeros_like(hidden))
        return hidden, k_out, v_out

    in_specs = (rows_spec, full_spec, full_spec, full_spec, full_spec, full_spec, full_spec, pool_spec, pool_spec, table_spec, table_spec, vec_spec, vec_spec, vec_spec, vec_spec)
    return jax.shard_map(device_fn, mesh=mesh, in_specs=in_specs, out_specs=(rows_spec, pool_spec, pool_spec), check_vma=False)
```

profile of v0, /device:TPU:97, one launch (start us, length us, event | category | flops | bytes accessed | tf_op | source)
XLA Modules:
  0.0 466.3 jit_solution(14874250424278974150)
XLA Ops:
  0.6 0.7 broadcast_compare_fusion
  1.3 0.7 multiply_add_fusion.1
  2.1 0.4 convert_reduce_fusion
  2.4 0.7 multiply_add_fusion.2
  3.1 0.7 select_reduce_fusion.1.slot_ref
  3.8 4.8 %pack_pages.2 = bf16[32,1,2,16,16,128]{5,4,3,2,1,0:T(8,128)(2,1)} custom-call(s32[96]{0:T(128)} %select_reduce_fusion.1.slot_ref, bf16[72,2,16,16,128]{4,3,2,1,0:T(8,128)(2,1)} %k_ref.5, bf16[72,2,16,16,128]{4,3,2,1,0:T(8,128)(2,1)} %v_ref.5), custom_call_target="tpu_custom_call" | custom-call | flops 100000000 | bytes 2097152 | tf_op jit(solution)/shard_map/pack_pages/pallas_call | solution.py:85
  8.7 8.7 %all-to-all-start = ((bf16[32,1,2,16,16,128]{5,4,3,2,1,0:T(8,128)(2,1)}), bf16[32,1,2,16,16,128]{5,4,3,2,1,0:T(8,128)(2,1)}, u32[]{:S(2)}, u32[]{:S(2)}) async-start(bf16[32,1,2,16,16,128]{5,4,3,2,1,0:T(8,128)(2,1)} %pack_pages.2), calls=%async_computation | async-start | bytes 8388608 | tf_op jit(solution)/shard_map/all_to_all | solution.py:642
  17.5 4.6 fusion.67
  22.1 4.6 fusion.64
  26.7 4.6 fusion.61
  31.3 14.5 %pack_pages.3 = (bf16[32,1,2,16,16,128]{5,4,3,2,1,0:T(8,128)(2,1)}, bf16[32,2,2,16,16,128]{5,4,3,2,1,0:T(8,128)(2,1)}, bf16[32,1,2,16,16,128]{5,4,3,2,1,0:T(8,128)(2,1)}, bf16[32,1,2,16,16,128]{5,4,3,2,1,0:T(8,128)(2,1)}) custom-call(s32[96]{0:T(128)} %select_reduce_fusion.1.slot_ref, bf16[72,2,16,16,128]{4,3,2,1,0:T(8,128)(2,1)} %k_ref.5, ...), custom_call_target="tpu_custom_call" | custom-call | flops 500000000 | bytes 10485760 | tf_op jit(solution)/shard_map/pack_pages/pallas_call | solution.py:85
  45.8 0.6 select_reduce_fusion.2.from_ref
  46.4 15.3 %keep_pages.1 = (bf16[72,2,16,16,128]{4,3,2,1,0:T(8,128)(2,1)}, bf16[72,2,16,16,128]{4,3,2,1,0:T(8,128)(2,1)}) custom-call(s32[72]{0:T(128)} %select_reduce_fusion.2.from_ref, bf16[72,2,16,16,128]{4,3,2,1,0:T(8,128)(2,1)} %k_ref.5, bf16[72,2,16,16,128]{4,3,2,1,0:T(8,128)(2,1)} %v_ref.5), custom_call_target="tpu_custom_call" | custom-call | flops 1000000000 | bytes 33554432 | tf_op jit(solution)/shard_map/keep_pages/pallas_call | solution.py:123
  61.8 0.7 pad_maximum_fusion.x_ref
  62.5 34.9 %spread_queries.2.x_ref.rest_2_.rest_1_ = bf16[2,16,3,4,32,128]{5,4,3,2,1,0:T(8,128)(2,1)} custom-call(bf16[3,4,32,128]{3,2,1,0:T(8,128)(2,1)} %pad_maximum_fusion.x_ref), custom_call_target="tpu_custom_call" | custom-call | tf_op jit(solution)/shard_map/spread_queries/pallas_call | solution.py:419
  97.4 4.6 all-to-all-start.1
  102.0 0.1 copy.30
  102.1 0.1 sub.83
  102.4 0.1 min.12
  102.5 0.7 select_reduce_fusion.code_ref
  103.2 14.1 %attend_pages.2.acc_ref = f32[2,16,5,32,128]{4,3,2,1,0:T(8,128)} custom-call(s32[72]{0:T(128)} %select_reduce_fusion.code_ref, bf16[2,16,3,4,32,128]{5,4,3,2,1,0:T(8,128)(2,1)} %spread_queries.2.x_ref.rest_2_.rest_1_, bf16[72,2,16,16,128]{4,3,2,1,0:T(8,128)(2,1)} %k_ref.5, bf16[72,2,16,16,128]{4,3,2,1,0:T(8,128)(2,1)} %v_ref.5), custom_call_target="tpu_custom_call" | custom-call | flops 1000000000 | bytes 9437184 | tf_op jit(solution)/shard_map/attend_pages/pallas_call | solution.py:318
  117.2 8.5 %merge_chip.2.sums_ref = f32[16,5,32,128]{3,2,1,0:T(8,128)} custom-call(f32[2,16,5,32,128]{4,3,2,1,0:T(8,128)} %attend_pages.2.acc_ref), custom_call_target="tpu_custom_call" | custom-call | flops 1000000000 | bytes 8388608 | tf_op jit(solution)/shard_map/merge_chip/pallas_call | solution.py:476
  125.8 49.3 %gather_home.2 = bf16[4,32,128]{2,1,0:T(8,128)(2,1)} custom-call(f32[16,5,32,128]{3,2,1,0:T(8,128)} %merge_chip.2.sums_ref, bf16[3,4,32,128]{3,2,1,0:T(8,128)(2,1)} %pad_maximum_fusion.x_ref), custom_call_target="tpu_custom_call" | custom-call | tf_op jit(solution)/shard_map/gather_home/pallas_call | solution.py:581
  175.1 7.2 %all-to-all-start.3 = ((bf16[32,2,2,16,16,128]{5,4,3,2,1,0:T(8,128)(2,1)}), bf16[32,2,2,16,16,128]{5,4,3,2,1,0:T(8,128)(2,1)}, u32[]{:S(2)}, u32[]{:S(2)}) async-start(bf16[32,2,2,16,16,128]{5,4,3,2,1,0:T(8,128)(2,1)} %get-tuple-element.59), calls=%async_computation.3 | async-start | bytes 16777216 | tf_op jit(solution)/shard_map/all_to_all | solution.py:642
  182.4 4.6 fusion.58
  186.9 22.7 %fusion.52 = bf16[8,2048]{1,0:T(8,128)(2,1)S(1)} fusion(bf16[2,8192,2048]{2,1,0:T(8,128)(2,1)} %param.21, bf16[8,2048]{1,0:T(8,128)(2,1)S(1)} %fusion.58, bf16[2,2048,8192]{2,1,0:T(8,128)(2,1)} %param.20), kind=kOutput, calls=%fused_computation.44 | convolution fusion | flops 537509888 | bytes 67207168 | tf_op jit(solution)/shard_map/dot_general | solution.py:676
  209.6 4.6 fusion.76
  214.2 4.6 fusion.73
  218.9 4.6 fusion.70
  223.5 0.7 subtract_bitcast_fusion.1
  224.2 0.1 select_reduce_fusion.3
  224.3 0.7 pad_maximum_fusion.1.x_ref
  225.0 0.5 compare_select_fusion.offset_ref
  225.5 0.5 compare_select_fusion.2.first_ref
  226.1 3.9 place_pages.3
  230.0 85.9 %spread_queries.3.x_ref.rest_3_.rest_2_ = bf16[2,16,3,4,32,128]{5,4,3,2,1,0:T(8,128)(2,1)} custom-call(bf16[3,4,32,128]{3,2,1,0:T(8,128)(2,1)} %pad_maximum_fusion.1.x_ref), custom_call_target="tpu_custom_call" | custom-call | tf_op jit(solution)/shard_map/spread_queries/pallas_call | solution.py:419
  315.9 6.3 %all-to-all-start.4 = ((bf16[32,1,2,16,16,128]{5,4,3,2,1,0:T(8,128)(2,1)}), bf16[32,1,2,16,16,128]{5,4,3,2,1,0:T(8,128)(2,1)}, u32[]{:S(2)}, u32[]{:S(2)}) async-start(bf16[32,1,2,16,16,128]{5,4,3,2,1,0:T(8,128)(2,1)} %get-tuple-element.60), calls=%async_computation.4 | async-start | bytes 8388608 | tf_op jit(solution)/shard_map/all_to_all | solution.py:642
  322.3 14.1 %attend_pages.3.acc_ref = f32[2,16,5,32,128]{4,3,2,1,0:T(8,128)} custom-call(s32[72]{0:T(128)} %select_reduce_fusion.code_ref, bf16[2,16,3,4,32,128]{5,4,3,2,1,0:T(8,128)(2,1)} %spread_queries.3.x_ref.rest_3_.rest_2_, bf16[72,2,16,16,128]{4,3,2,1,0:T(8,128)(2,1)} %k_ref.5, bf16[72,2,16,16,128]{4,3,2,1,0:T(8,128)(2,1)} %v_ref.5), custom_call_target="tpu_custom_call" | custom-call | flops 1000000000 | bytes 9437184 | tf_op jit(solution)/shard_map/attend_pages/pallas_call | solution.py:318
  336.5 8.5 %merge_chip.3.sums_ref = f32[16,5,32,128]{3,2,1,0:T(8,128)} custom-call(f32[2,16,5,32,128]{4,3,2,1,0:T(8,128)} %attend_pages.3.acc_ref), custom_call_target="tpu_custom_call" | custom-call | flops 1000000000 | bytes 8388608 | tf_op jit(solution)/shard_map/merge_chip/pallas_call | solution.py:476
  345.0 49.0 %gather_home.3 = bf16[4,32,128]{2,1,0:T(8,128)(2,1)} custom-call(f32[16,5,32,128]{3,2,1,0:T(8,128)} %merge_chip.3.sums_ref, bf16[3,4,32,128]{3,2,1,0:T(8,128)(2,1)} %pad_maximum_fusion.1.x_ref), custom_call_target="tpu_custom_call" | custom-call | tf_op jit(solution)/shard_map/gather_home/pallas_call | solution.py:581
  394.0 0.8 reshape.80
  394.7 4.6 fusion.55
  399.3 7.6 %all-to-all-start.2 = ((bf16[32,1,2,16,16,128]{5,4,3,2,1,0:T(8,128)(2,1)}), bf16[32,1,2,16,16,128]{5,4,3,2,1,0:T(8,128)(2,1)}, u32[]{:S(2)}, u32[]{:S(2)}) async-start(bf16[32,1,2,16,16,128]{5,4,3,2,1,0:T(8,128)(2,1)} %get-tuple-element.58), calls=%async_computation.2 | async-start | bytes 8388608 | tf_op jit(solution)/shard_map/all_to_all | solution.py:642
  407.0 22.7 %fusion.49 = bf16[8,2048]{1,0:T(8,128)(2,1)S(1)} fusion(bf16[2,8192,2048]{2,1,0:T(8,128)(2,1)} %param.21, bf16[8,2048]{1,0:T(8,128)(2,1)S(1)} %fusion.55, bf16[2,2048,8192]{2,1,0:T(8,128)(2,1)} %param.20), kind=kOutput, calls=%fused_computation.43 | convolution fusion | flops 537509888 | bytes 67207168 | tf_op jit(solution)/shard_map/dot_general | solution.py:676
  429.7 0.7 bitcast_select_fusion
  430.4 10.0 %place_pages.4 = (bf16[72,2,16,16,128]{4,3,2,1,0:T(8,128)(2,1)}, bf16[72,2,16,16,128]{4,3,2,1,0:T(8,128)(2,1)}) custom-call(s32[72]{0:T(128)} %select_reduce_fusion.2.from_ref, s32[72]{0:T(128)} %compare_select_fusion.2.first_ref, s32[72]{0:T(128)} %copy-done.3, s32[128]{0:T(128)} %compare_select_fusion.offset_ref, ...), custom_call_target="tpu_custom_call", output_to_operand_aliasing={{0}: (8, {}), {1}: (9, {})} | custom-call | flops 400000000 | bytes 8388608 | tf_op jit(solution)/shard_map/place_pages/pallas_call | solution.py:241
  440.4 20.2 %all-to-all-done.2.rest_0_ = bf16[32,1,2,16,16,128]{5,4,3,2,1,0:T(8,128)(2,1)} async-done(((bf16[32,1,2,16,16,128]{5,4,3,2,1,0:T(8,128)(2,1)}), bf16[32,1,2,16,16,128]{5,4,3,2,1,0:T(8,128)(2,1)}, u32[]{:S(2)}, u32[]{:S(2)}) %all-to-all-start.2) | async-done | bytes 4194336 | tf_op jit(solution)/shard_map/all_to_all | solution.py:642
  460.7 5.4 %place_pages.5 = (bf16[72,2,16,16,128]{4,3,2,1,0:T(8,128)(2,1)}, bf16[72,2,16,16,128]{4,3,2,1,0:T(8,128)(2,1)}) custom-call(s32[72]{0:T(128)} %select_reduce_fusion.2.from_ref, s32[72]{0:T(128)} %compare_select_fusion.2.first_ref, s32[72]{0:T(128)} %copy-done.3, s32[128]{0:T(128)} %compare_select_fusion.offset_ref, ...), custom_call_target="tpu_custom_call", output_to_operand_aliasing={{0}: (7, {}), {1}: (8, {})} | custom-call | flops 200000000 | bytes 4194304 | tf_op jit(solution)/shard_map/place_pages/pallas_call | solution.py:241
  (36 shorter events, 0.5 us)
Async XLA Ops:
  3.8 13.6 %copy-start.1 = (bf16[2,4,2048]{2,1,0:T(4,128)(2,1)S(1)}, bf16[2,4,2048]{2,1,0:T(4,128)(2,1)}, u32[]{:S(2)}) copy-start(bf16[2,4,2048]{2,1,0:T(4,128)(2,1)} %param.15) | copy-start | bytes 98308
  8.7 88.7 %all-to-all-start = ((bf16[32,1,2,16,16,128]{5,4,3,2,1,0:T(8,128)(2,1)}), bf16[32,1,2,16,16,128]{5,4,3,2,1,0:T(8,128)(2,1)}, u32[]{:S(2)}, u32[]{:S(2)}) async-start(bf16[32,1,2,16,16,128]{5,4,3,2,1,0:T(8,128)(2,1)} %pack_pages.2), calls=%async_computation | async-start | bytes 8388608 | tf_op jit(solution)/shard_map/all_to_all | solution.py:642
  61.8 40.2 %copy-start.4 = (s32[128,12]{0,1:T(8,128)S(1)}, s32[128,12]{0,1:T(8,128)}, u32[]{:S(2)}) copy-start(s32[128,12]{0,1:T(8,128)} %param.24) | copy-start | bytes 18436
  61.8 40.5 %copy-start.5 = (s32[128]{0:T(128)S(1)}, s32[128]{0:T(128)}, u32[]{:S(2)}) copy-start(s32[128]{0:T(128)} %param.26) | copy-start | bytes 1540
  97.4 77.7 %all-to-all-start.1 = ((bf16[32,1,2,16,16,128]{5,4,3,2,1,0:T(8,128)(2,1)}), bf16[32,1,2,16,16,128]{5,4,3,2,1,0:T(8,128)(2,1)}, u32[]{:S(2)}, u32[]{:S(2)}) async-start(bf16[32,1,2,16,16,128]{5,4,3,2,1,0:T(8,128)(2,1)} %get-tuple-element.46), calls=%async_computation.1 | async-start | bytes 8388608 | tf_op jit(solution)/shard_map/all_to_all | solution.py:642
  175.1 7.3 %copy-start = (bf16[4,32,128]{2,1,0:T(8,128)(2,1)S(1)}, bf16[4,32,128]{2,1,0:T(8,128)(2,1)}, u32[]{:S(2)}) copy-start(bf16[4,32,128]{2,1,0:T(8,128)(2,1)} %gather_home.2) | copy-start | bytes 98308
  175.1 140.8 %all-to-all-start.3 = ((bf16[32,2,2,16,16,128]{5,4,3,2,1,0:T(8,128)(2,1)}), bf16[32,2,2,16,16,128]{5,4,3,2,1,0:T(8,128)(2,1)}, u32[]{:S(2)}, u32[]{:S(2)}) async-start(bf16[32,2,2,16,16,128]{5,4,3,2,1,0:T(8,128)(2,1)} %get-tuple-element.59), calls=%async_computation.3 | async-start | bytes 16777216 | tf_op jit(solution)/shard_map/all_to_all | solution.py:642
  214.2 9.3 %copy-start.6 = (s32[128]{0:T(128)S(1)}, s32[128]{0:T(128)}, u32[]{:S(2)}) copy-start(s32[128]{0:T(128)} %param.27) | copy-start | bytes 1540
  214.2 11.3 %copy-start.2 = (s32[72]{0:T(128)S(1)}, s32[72]{0:T(128)}, u32[]{:S(2)}) copy-start(s32[72]{0:T(128)} %select_reduce_fusion.2.from_ref) | copy-start | bytes 868
  224.3 1.7 copy-start.3
  315.9 83.4 %all-to-all-start.4 = ((bf16[32,1,2,16,16,128]{5,4,3,2,1,0:T(8,128)(2,1)}), bf16[32,1,2,16,16,128]{5,4,3,2,1,0:T(8,128)(2,1)}, u32[]{:S(2)}, u32[]{:S(2)}) async-start(bf16[32,1,2,16,16,128]{5,4,3,2,1,0:T(8,128)(2,1)} %get-tuple-element.60), calls=%async_computation.4 | async-start | bytes 8388608 | tf_op jit(solution)/shard_map/all_to_all | solution.py:642
  399.3 61.4 %all-to-all-start.2 = ((bf16[32,1,2,16,16,128]{5,4,3,2,1,0:T(8,128)(2,1)}), bf16[32,1,2,16,16,128]{5,4,3,2,1,0:T(8,128)(2,1)}, u32[]{:S(2)}, u32[]{:S(2)}) async-start(bf16[32,1,2,16,16,128]{5,4,3,2,1,0:T(8,128)(2,1)} %get-tuple-element.58), calls=%async_computation.2 | async-start | bytes 8388608 | tf_op jit(solution)/shard_map/all_to_all | solution.py:642
where the time goes:
time: 471 us; the launch traced here: 466 us
  Pallas kernels  318 us (68%)
  matrix products  82 us (17%)
  starting transfers between devices  34.5 us (7%)
  waiting for transfers between devices  20.2 us (4%)
  other arithmetic  8.54 us (2%)
    pallas_call x2, Pallas kernels, spread(): pl.pallas_call(functools.partial(spread_kernel, n), out_shape=jax.ShapeDt...  121 us
    pallas_call x2, Pallas kernels, gather_home(): pl.pallas_call(functools.partial(gather_home_kernel, n, x.shape[-1] ** (-...  98.3 us
    dot_general x2, matrix products, device_fn(): jnp.dot(inner, w_down[layer], preferred_element_type=jnp.float32)  45.4 us
    all_to_all x5, starting transfers between devices, exchange(): return lax.all_to_all(block, 'kv', 0, 0, tiled=True)  34.5 us
    pallas_call x2, Pallas kernels, attend_pages(): pl.pallas_call(functools.partial(attend_kernel, block, pages_seq, seq_dev...  28.2 us
    dot_general x6, matrix products, device_fn(): jnp.dot(hidden, w[layer], preferred_element_type=jnp.float32)  27.4 us
    all_to_all x5, waiting for transfers between devices, exchange(): return lax.all_to_all(block, 'kv', 0, 0, tiled=True)  20.2 us
    pallas_call x3, Pallas kernels, place_pages(): pl.pallas_call(functools.partial(place_kernel, depth, lead, plan, patches...  19.4 us
  transfers between devices with their start and end apart: 5, of which 1 were waited for; matrix products, arithmetic and copies ran while one was open for 19% of the time, Pallas kernels for 66%

commit v1 on v0

--- a/solution.py
+++ b/solution.py
@@ -334,20 +334,26 @@
     me = lax.axis_index("kv")
     chips = n // 2
     core, chip = lax.rem(me, 2), me // 2
+    barrier = pltpu.get_barrier_semaphore()
+
+    def greet(j, carry):
+        pl.semaphore_signal(barrier, inc=1, device_id={"kv": 2 * lax.rem(chip + j, chips) + core}, device_id_type=MESH)
+        return carry
+
+    lax.fori_loop(1, chips, greet, 0)
+    pl.semaphore_signal(barrier, inc=1, device_id={"kv": me + 1 - 2 * core}, device_id_type=MESH)
+    pl.semaphore_wait(barrier, chips)
+    spread_body(n, x_ref, out_ref, held, send_sem, recv_sem, pass_sem, got_sem, copy_sem)
+
+
+def spread_body(n, x_ref, out_ref, held, send_sem, recv_sem, pass_sem, got_sem, copy_sem):
+    me = lax.axis_index("kv")
+    chips = n // 2
+    core, chip = lax.rem(me, 2), me // 2
     other = me + 1 - 2 * core
 
     def peer(j):
         return 2 * lax.rem(chip + j, chips) + core
-
-    barrier = pltpu.get_barrier_semaphore()
-
-    def greet(j, carry):
-        pl.semaphore_signal(barrier, inc=1, device_id={"kv": peer(j)}, device_id_type=MESH)
-        return carry
-
-    lax.fori_loop(1, chips, greet, 0)
-    pl.semaphore_signal(barrier, inc=1, device_id={"kv": other}, device_id_type=MESH)
-    pl.semaphore_wait(barrier, chips)
 
     def send(j):
         return pltpu.make_async_remote_copy(
@@ -489,24 +495,59 @@
     )(acc)
 
 
-def gather_home_kernel(n, scale, sums_ref, x_ref, o_ref, held, send_sem, recv_sem):
+def layer_kernel(n, scale, layer, follow, *refs):
+    sums_ref, x_ref, hid_ref, chunk_ref, wo_ref, wu_ref, wd_ref = refs[:7]
+    refs = refs[7:]
+    if follow:
+        proj, refs = refs[:3], refs[3:]
+    hid_out, got_ref = refs[:2]
+    refs = refs[2:]
+    if follow:
+        x_out, all_out = refs[:2]
+        refs = refs[2:]
+    held, o_scr, rows_scr, mid_scr, acc_scr, wide, up, down, wide_sem, up_sem, down_sem, send_sem, recv_sem, page_send, page_recv = refs[:15]
+    refs = refs[15:]
     me = lax.axis_index("kv")
     _, seq_dev, rows, head_dim = x_ref.shape
     heads = rows // 2
     chips = n // 2
     core, chip = lax.rem(me, 2), me // 2
+    hid_rows, width = hid_ref.shape
+    tile, up_tile = wide.shape[2], up.shape[2]
+    wide_slots, up_slots = wide.shape[0], up.shape[0]
+    n_wide, n_up = width // tile, wu_ref.shape[2] // up_tile
 
     def peer(j):
         return 2 * lax.rem(chip + j, chips) + core
 
+    def anyone(j):
+        return lax.rem(me + j, n)
+
     barrier = pltpu.get_barrier_semaphore()
 
     def greet(j, carry):
-        pl.semaphore_signal(barrier, inc=1, device_id={"kv": peer(j)}, device_id_type=MESH)
-        return carry
-
-    lax.fori_loop(1, chips, greet, 0)
-    pl.semaphore_wait(barrier, chips - 1)
+        pl.semaphore_signal(barrier, inc=1, device_id={"kv": anyone(j)}, device_id_type=MESH)
+        return carry
+
+    lax.fori_loop(1, n, greet, 0)
+
+    def wide_copy(w, at, t, slot):
+        return pltpu.make_async_copy(w.at[at, :, pl.ds(pl.multiple_of(t * tile, tile), tile)], wide.at[slot], wide_sem.at[slot])
+
+    def up_copy(t):
+        slot = lax.rem(t, up_slots)
+        return pltpu.make_async_copy(wu_ref.at[layer, :, pl.ds(pl.multiple_of(t * up_tile, up_tile), up_tile)], up.at[slot], up_sem.at[slot])
+
+    def down_copy(t):
+        slot = lax.rem(t, up_slots)
+        return pltpu.make_async_copy(wd_ref.at[layer, pl.ds(pl.multiple_of(t * up_tile, up_tile), up_tile)], down.at[slot], down_sem.at[slot])
+
+    for t in range(n_wide):
+        wide_copy(wo_ref, layer, t, t).start()
+    for t in range(up_slots):
+        up_copy(t).start()
+        down_copy(t).start()
+    pl.semaphore_wait(barrier, n - 1)
 
     def send(j):
         return pltpu.make_async_remote_copy(
@@ -514,11 +555,23 @@
             device_id={"kv": peer(j)}, device_id_type=MESH,
         )
 
+    def send_pages(j):
+        return pltpu.make_async_remote_copy(
+            src_ref=chunk_ref.at[anyone(j)], dst_ref=got_ref.at[me], send_sem=page_send.at[j], recv_sem=page_recv.at[me],
+            device_id={"kv": anyone(j)}, device_id_type=MESH,
+        )
+
     def start(j, carry):
         send(j).start()
         return carry
 
     lax.fori_loop(1, chips, start, 0)
+
+    def start_pages(j, carry):
+        send_pages(j).start()
+        return carry
+
+    lax.fori_loop(1, n, start_pages, 0)
     held[chip] = sums_ref[chip]
 
     queries = [x_ref[0, i].astype(jnp.float32) for i in range(seq_dev)]
@@ -533,6 +586,7 @@
         jnp.where(second_row, jnp.sum(queries[i] * twice(0, i, 1), axis=1, keepdims=True) * scale, LOW)
         for i in range(seq_dev)
     ]
+
     def arrive(j, carry):
         at = lax.rem(chip + chips - j, chips)
         pltpu.make_async_remote_copy(
@@ -567,7 +621,60 @@
 
     totals, mixed = lax.fori_loop(0, chips, merge, (tuple(totals), tuple(mixed)))
     for i in range(seq_dev):
-        o_ref[i] = (mixed[i] / totals[i]).astype(o_ref.dtype)
+        o_scr[i * rows:(i + 1) * rows] = (mixed[i] / totals[i]).astype(jnp.bfloat16).astype(jnp.float32)
+    for h in range(heads):
+        rows_scr[:, h * head_dim:(h + 1) * head_dim] = o_scr[pl.ds(h, hid_rows, stride=heads), :].astype(jnp.bfloat16)
+
+    def add_out(t, carry):
+        wide_copy(wo_ref, layer, t, t).wait()
+        cut = pl.ds(pl.multiple_of(t * tile, tile), tile)
+        part = jnp.dot(rows_scr[...], wide[t], preferred_element_type=jnp.float32)
+        mid_scr[:, cut] = (hid_ref[:, cut].astype(jnp.float32) + part).astype(jnp.bfloat16)
+        return carry
+
+    lax.fori_loop(0, n_wide, add_out, 0)
+    if follow:
+        for t in range(wide_slots):
+            wide_copy(proj[t // n_wide], layer + 1, t % n_wide, t).start()
+    acc_scr[...] = jnp.zeros_like(acc_scr)
+
+    def mlp(t, carry):
+        slot = lax.rem(t, up_slots)
+        up_copy(t).wait()
+        inner = jax.nn.gelu(jnp.dot(mid_scr[...], up[slot], preferred_element_type=jnp.float32)).astype(jnp.bfloat16)
+        down_copy(t).wait()
+        acc_scr[...] += jnp.dot(inner, down[slot], preferred_element_type=jnp.float32)
+
+        @pl.when(t + up_slots < n_up)
+        def _():
+            up_copy(t + up_slots).start()
+            down_copy(t + up_slots).start()
+
+        return carry
+
+    lax.fori_loop(0, n_up, mlp, 0)
+    hid_out[...] = (mid_scr[...].astype(jnp.float32) + acc_scr[...]).astype(jnp.bfloat16)
+
+    if follow:
+        xs, all_held, pass_send, pass_recv, spread_send, spread_recv, copy_sem = refs
+        other = me + 1 - 2 * core
+        for m in range(3):
+            def project(t, carry):
+                slot = lax.rem(m * n_wide + t, wide_slots)
+                wide_copy(proj[m], layer + 1, t, slot).wait()
+                part = jnp.dot(hid_out[...], wide[slot], preferred_element_type=jnp.float32)
+                acc_scr[:, pl.ds(pl.multiple_of(t * tile, tile), tile)] = part
+                if m < 2:
+                    wide_copy(proj[m + 1], layer + 1, t, slot).start()
+                return carry
+
+            lax.fori_loop(0, n_wide, project, 0)
+            for h in range(heads):
+                o_scr[pl.ds(h, hid_rows, stride=heads), :] = acc_scr[:, h * head_dim:(h + 1) * head_dim]
+            for i in range(seq_dev):
+                xs[m, i] = o_scr[i * rows:(i + 1) * rows].astype(jnp.bfloat16)
+        x_out[...] = xs[...]
+        spread_body(n, xs, all_out, all_held, spread_send, spread_recv, pass_send, pass_recv, copy_sem)
 
     def finish(j, carry):
         send(j).wait_send()
@@ -575,22 +682,60 @@
 
     lax.fori_loop(1, chips, finish, 0)
 
-
-def gather_home(sums, x, n):
+    def pages_came(j, carry):
+        at = lax.rem(me + n - j, n)
+        pltpu.make_async_remote_copy(
+            src_ref=chunk_ref.at[at], dst_ref=got_ref.at[at], send_sem=page_send.at[j], recv_sem=page_recv.at[at],
+            device_id={"kv": anyone(j)}, device_id_type=MESH,
+        ).wait_recv()
+        send_pages(j).wait_send()
+        return carry
+
+    lax.fori_loop(1, n, pages_came, 0)
+
+
+def end_layer(sums, x, hidden, chunk, w_out, w_up, w_down, proj, layer, n):
     chips = n // 2
+    hid_rows, width = hidden.shape
+    seq_dev, rows, head_dim = x.shape[1:]
+    follow = bool(proj)
+    tile, up_slots = 512, 3
+    wide_slots = width // tile
+    out_shape = [jax.ShapeDtypeStruct(hidden.shape, hidden.dtype), jax.ShapeDtypeStruct(chunk.shape, chunk.dtype)]
+    out_specs = [VMEM, ANY]
+    scratch = [
+        pltpu.VMEM(sums.shape, sums.dtype),
+        pltpu.VMEM((seq_dev * rows, head_dim), jnp.float32),
+        pltpu.VMEM(hidden.shape, jnp.bfloat16),
+        pltpu.VMEM(hidden.shape, jnp.bfloat16),
+        pltpu.VMEM(hidden.shape, jnp.float32),
+        pltpu.VMEM((wide_slots, width, tile), w_out.dtype),
+        pltpu.VMEM((up_slots, width, tile), w_up.dtype),
+        pltpu.VMEM((up_slots, tile, width), w_down.dtype),
+        pltpu.SemaphoreType.DMA((wide_slots,)),
+        pltpu.SemaphoreType.DMA((up_slots,)),
+        pltpu.SemaphoreType.DMA((up_slots,)),
+        pltpu.SemaphoreType.DMA((chips,)),
+        pltpu.SemaphoreType.DMA((chips,)),
+        pltpu.SemaphoreType.DMA((n,)),
+        pltpu.SemaphoreType.DMA((n,)),
+    ]
+    if follow:
+        spread_shape = (2, chips) + x.shape
+        out_shape += [jax.ShapeDtypeStruct(x.shape, x.dtype), jax.ShapeDtypeStruct(spread_shape, x.dtype)]
+        out_specs += [VMEM, ANY]
+        scratch += [pltpu.VMEM(x.shape, x.dtype), pltpu.VMEM(spread_shape, x.dtype)]
+        scratch += [pltpu.SemaphoreType.DMA((chips,))] * 4 + [pltpu.SemaphoreType.DMA((n,))]
     return pl.pallas_call(
-        functools.partial(gather_home_kernel, n, x.shape[-1] ** -0.5),
-        out_shape=jax.ShapeDtypeStruct(x.shape[1:], jnp.bfloat16),
-        in_specs=[VMEM] * 2,
-        out_specs=VMEM,
-        scratch_shapes=[
-            pltpu.VMEM(sums.shape, sums.dtype),
-            pltpu.SemaphoreType.DMA((chips,)),
-            pltpu.SemaphoreType.DMA((chips,)),
-        ],
-        compiler_params=pltpu.CompilerParams(collective_id=1, has_side_effects=True),
-        name="gather_home",
-    )(sums, x)
+        functools.partial(layer_kernel, n, head_dim ** -0.5, layer, follow),
+        out_shape=out_shape,
+        in_specs=[VMEM] * 3 + [ANY] * (4 + len(proj)),
+        out_specs=out_specs,
+        scratch_shapes=scratch,
+        compiler_params=pltpu.CompilerParams(collective_id=3 + layer, has_side_effects=True),
+        cost_estimate=pl.CostEstimate(flops=10 ** 10, bytes_accessed=2 ** 27, transcendentals=0),
+        name="end_layer",
+    )(sums, x, hidden, chunk, w_out, w_up, w_down, *proj)
 
 
 def solution(mesh):
@@ -655,30 +800,27 @@
         k_out, v_out = keep_pages(from_page, k_pool, v_pool)
 
         hidden = jnp.transpose(embeds, (1, 0, 2)).reshape(seq_dev * steps, width)
+        x = jnp.stack([
+            jnp.dot(hidden, w[0], preferred_element_type=jnp.float32).astype(jnp.bfloat16).reshape(seq_dev, steps * heads, head_dim)
+            for w in (w_query, w_key, w_value)
+        ])
+        x, k_out, v_out, packed = lax.optimization_barrier((x, k_out, v_out, packed))
+        x_all = spread(x, groups)
         rows = []
         for layer in range(n_layers):
-            x = jnp.stack([
-                jnp.dot(hidden, w[layer], preferred_element_type=jnp.float32).astype(jnp.bfloat16).reshape(seq_dev, steps * heads, head_dim)
-                for w in (w_query, w_key, w_value)
-            ])
-            x, k_out, v_out, packed = lax.optimization_barrier((x, k_out, v_out, packed))
-            x_all = spread(x, groups)
             rows.append(x_all)
             x_all = send_next(x_all, 1)
-            acc = attend_pages(code, x_all, k_pool, v_pool, layer, pages_seq)
-            mixed = gather_home(merge_chip(acc), x, groups)
-            mixed = send_next(mixed, 1 if layer + 1 < n_layers else len(plan))
-            if layer == 0:
-                k_out, v_out = place_pages(plan[:2], (), seq_dev, *tables, got[:2], [], k_out, v_out)
-            mixed = mixed.reshape(seq_dev * steps, heads * head_dim)
-            hidden = (hidden.astype(jnp.float32) + jnp.dot(mixed, w_out[layer], preferred_element_type=jnp.float32)).astype(jnp.bfloat16)
-            inner = jax.nn.gelu(jnp.dot(hidden, w_up[layer], preferred_element_type=jnp.float32)).astype(jnp.bfloat16)
-            hidden = (hidden.astype(jnp.float32) + jnp.dot(inner, w_down[layer], preferred_element_type=jnp.float32)).astype(jnp.bfloat16)
-        last_round = (rounds - 1,)
-        k_out, v_out = place_pages(
-            plan[2:-1], ((0, (), False), (1, last_round, False)), seq_dev, *tables, got[2:-1], rows, k_out, v_out
-        )
-        k_out, v_out = place_pages(plan[-1:], ((1, last_round, True),), seq_dev, *tables, got[-1:], rows, k_out, v_out)
+            sums = merge_chip(attend_pages(code, x_all, k_pool, v_pool, layer, pages_seq))
+            if layer:
+                k_out, v_out = place_pages(plan[:3], (), seq_dev, *tables, got[:3], [], k_out, v_out)
+                sums, k_out, v_out = lax.optimization_barrier((sums, k_out, v_out))
+            follow = (w_query, w_key, w_value) if layer + 1 < n_layers else ()
+            hidden, pages, *ahead = end_layer(sums, x, hidden, packed[len(got)], w_out, w_up, w_down, follow, layer, groups)
+            got.append(pages)
+            if ahead:
+                x, x_all = ahead
+        everything = ((0, (), False), (1, (), False))
+        k_out, v_out = place_pages(plan[3:], everything, seq_dev, *tables, got[3:], rows, k_out, v_out)
         hidden = jnp.transpose(hidden.reshape(seq_dev, steps, width), (1, 0, 2))
         done = lax.dynamic_slice(finished, (me * seq_dev,), (seq_dev,)) != 0
         live = jnp.stack([jnp.ones_like(done), ~done])

time: 471 us -> 498 us (1.057)
  Pallas kernels: 318 us -> 448 us
  matrix products: 82 us -> 13.7 us
  waiting for transfers between devices: 20.2 us -> 0.01 us
  starting transfers between devices: 34.5 us -> 17.3 us
    pallas_call x2, Pallas kernels: 98.3 us -> 319 us  [end_layer(): pl.pallas_call(functools.partial(layer_kernel, n, head_dim ** (-0.5), lay...]
    pallas_call x2 -> x1, Pallas kernels: 121 us -> 34 us  [spread(): pl.pallas_call(functools.partial(spread_kernel, n), out_shape=jax.ShapeDt...]
    dot_general x10 -> x3, matrix products: 82 us -> 13.7 us  [device_fn(): jnp.dot(hidden, w[0], preferred_element_type=jnp.float32)]
    all_to_all x5 -> x3, waiting for transfers between devices: 20.2 us -> 0.01 us  [exchange(): return lax.all_to_all(block, 'kv', 0, 0, tiled=True)]
    all_to_all x5 -> x3, starting transfers between devices: 34.5 us -> 17.3 us  [exchange(): return lax.all_to_all(block, 'kv', 0, 0, tiled=True)]
    pallas_call x3 -> x2, Pallas kernels: 19.4 us -> 15.1 us  [place_pages(): pl.pallas_call(functools.partial(place_kernel, depth, lead, plan, patches...]
  transfers between devices with their start and end apart: 5 -> 3, of which waited for: 1 -> 0; matrix products, arithmetic and copies ran while one was open for 19% -> 4% of each run, Pallas kernels for 66% -> 89%
where the time goes in v1:
time: 498 us; the launch traced here: 489 us
  Pallas kernels  448 us (90%)
  starting transfers between devices  17.3 us (3%)
  matrix products  13.7 us (3%)
  other arithmetic  8.09 us (2%)
    pallas_call x2, Pallas kernels, end_layer(): pl.pallas_call(functools.partial(layer_kernel, n, head_dim ** (-0.5), lay...  319 us
    pallas_call x1, Pallas kernels, spread(): pl.pallas_call(functools.partial(spread_kernel, n), out_shape=jax.ShapeDt...  34 us
    pallas_call x2, Pallas kernels, attend_pages(): pl.pallas_call(functools.partial(attend_kernel, block, pages_seq, seq_dev...  28.2 us
    pallas_call x2, Pallas kernels, pack_pages(): pl.pallas_call(functools.partial(pack_kernel, depth, lead, plan), out_sha...  19.2 us
    all_to_all x3, starting transfers between devices, exchange(): return lax.all_to_all(block, 'kv', 0, 0, tiled=True)  17.3 us
    pallas_call x2, Pallas kernels, merge_chip(): pl.pallas_call(merge_chip_kernel, out_shape=jax.ShapeDtypeStruct(blocks,...  17 us
    pallas_call x1, Pallas kernels, keep_pages(): pl.pallas_call(functools.partial(keep_kernel, depth, lead), out_shape=[ja...  15.3 us
    pallas_call x2, Pallas kernels, place_pages(): pl.pallas_call(functools.partial(place_kernel, depth, lead, plan, patches...  15.1 us
  transfers between devices with their start and end apart: 3, of which 0 were waited for; matrix products, arithmetic and copies ran while one was open for 4% of the time, Pallas kernels for 89%

profile of v1, /device:TPU:97, one launch (start us, length us, event | category | flops | bytes accessed | tf_op | source)
XLA Modules:
  0.0 488.9 jit_solution(16740566914128885577)
XLA Ops:
  0.6 0.7 broadcast_compare_fusion
  1.3 0.7 multiply_add_fusion.1
  2.1 0.4 convert_reduce_fusion
  2.4 0.7 multiply_add_fusion.2
  3.1 0.7 select_reduce_fusion.1.slot_ref
  3.8 4.7 pack_pages.2
  8.5 0.0 copy-start.1
  8.5 8.8 %all-to-all-start = ((bf16[32,1,2,16,16,128]{5,4,3,2,1,0:T(8,128)(2,1)}), bf16[32,1,2,16,16,128]{5,4,3,2,1,0:T(8,128)(2,1)}, u32[]{:S(2)}, u32[]{:S(2)}) async-start(bf16[32,1,2,16,16,128]{5,4,3,2,1,0:T(8,128)(2,1)} %pack_pages.2), calls=%async_computation | async-start | bytes 8388608 | tf_op jit(solution)/shard_map/all_to_all | solution.py:787
  17.4 0.0 copy-start
  17.4 4.6 fusion.16
  22.1 4.6 fusion.13
  26.7 0.0 copy-done
  26.7 4.6 fusion.10
  31.3 14.5 %pack_pages.3 = (bf16[32,1,2,16,16,128]{5,4,3,2,1,0:T(8,128)(2,1)}, bf16[32,2,2,16,16,128]{5,4,3,2,1,0:T(8,128)(2,1)}, bf16[32,1,2,16,16,128]{5,4,3,2,1,0:T(8,128)(2,1)}, bf16[32,1,2,16,16,128]{5,4,3,2,1,0:T(8,128)(2,1)}) custom-call(s32[96]{0:T(128)} %select_reduce_fusion.1.slot_ref, bf16[72,2,16,16,128]{4,3,2,1,0:T(8,128)(2,1)} %k_ref.5, ...), custom_call_target="tpu_custom_call" | custom-call | flops 500000000 | bytes 10485760 | tf_op jit(solution)/shard_map/pack_pages/pallas_call | solution.py:85
  45.8 0.7 select_reduce_fusion.2.from_ref
  46.4 15.3 %keep_pages.1 = (bf16[72,2,16,16,128]{4,3,2,1,0:T(8,128)(2,1)}, bf16[72,2,16,16,128]{4,3,2,1,0:T(8,128)(2,1)}) custom-call(s32[72]{0:T(128)} %select_reduce_fusion.2.from_ref, bf16[72,2,16,16,128]{4,3,2,1,0:T(8,128)(2,1)} %k_ref.5, bf16[72,2,16,16,128]{4,3,2,1,0:T(8,128)(2,1)} %v_ref.5), custom_call_target="tpu_custom_call" | custom-call | flops 1000000000 | bytes 33554432 | tf_op jit(solution)/shard_map/keep_pages/pallas_call | solution.py:123
  61.8 0.0 copy-start.4
  61.8 0.0 copy-start.5
  61.8 0.7 pad_maximum_fusion.x_ref.refs_1_
  62.5 34.0 %spread_queries.1.x_ref.rest_2_ = bf16[2,16,3,4,32,128]{5,4,3,2,1,0:T(8,128)(2,1)} custom-call(bf16[3,4,32,128]{3,2,1,0:T(8,128)(2,1)} %pad_maximum_fusion.x_ref.refs_1_), custom_call_target="tpu_custom_call" | custom-call | tf_op jit(solution)/shard_map/spread_queries/pallas_call | solution.py:425
  96.4 0.0 all-to-all-done.rest_0_
  96.4 4.4 all-to-all-start.1
  100.9 0.1 copy.27
  101.0 0.1 sub.78
  101.1 0.0 copy-done.5
  101.1 0.1 subtract_clamp_fusion
  101.2 0.1 min.12
  101.3 0.7 select_reduce_fusion.code_ref
  102.0 14.1 %attend_pages.2.acc_ref = f32[2,16,5,32,128]{4,3,2,1,0:T(8,128)} custom-call(s32[72]{0:T(128)} %select_reduce_fusion.code_ref, bf16[2,16,3,4,32,128]{5,4,3,2,1,0:T(8,128)(2,1)} %spread_queries.1.x_ref.rest_2_, bf16[72,2,16,16,128]{4,3,2,1,0:T(8,128)(2,1)} %k_ref.5, bf16[72,2,16,16,128]{4,3,2,1,0:T(8,128)(2,1)} %v_ref.5), custom_call_target="tpu_custom_call" | custom-call | flops 1000000000 | bytes 9437184 | tf_op jit(solution)/shard_map/attend_pages/pallas_call | solution.py:318
  116.1 8.5 %merge_chip.2.refs_0_ = f32[16,5,32,128]{3,2,1,0:T(8,128)} custom-call(f32[2,16,5,32,128]{4,3,2,1,0:T(8,128)} %attend_pages.2.acc_ref), custom_call_target="tpu_custom_call" | custom-call | flops 1000000000 | bytes 8388608 | tf_op jit(solution)/shard_map/merge_chip/pallas_call | solution.py:482
  124.6 218.1 %end_layer.2 = (bf16[8,2048]{1,0:T(8,128)(2,1)}, bf16[32,2,2,16,16,128]{5,4,3,2,1,0:T(8,128)(2,1)}, bf16[3,4,32,128]{3,2,1,0:T(8,128)(2,1)}, bf16[2,16,3,4,32,128]{5,4,3,2,1,0:T(8,128)(2,1)}) custom-call(f32[16,5,32,128]{3,2,1,0:T(8,128)} %merge_chip.2.refs_0_, bf16[3,4,32,128]{3,2,1,0:T(8,128)(2,1)} %pad_maximum_fusion.x_ref.refs_1_, ...), custom_call_target="tpu_custom_call" | custom-call | flops 10000000000 | bytes 134217728 | tf_op jit(solution)/shard_map/end_layer/pallas_call | solution.py:729
  342.7 0.0 copy-start.6
  342.7 0.0 all-to-all-done.1.rest_1_
  342.7 4.1 all-to-all-start.2
  346.8 0.0 copy-done.6
  346.8 0.1 not_bitcast_fusion
  346.9 14.1 %attend_pages.3.acc_ref = f32[2,16,5,32,128]{4,3,2,1,0:T(8,128)} custom-call(s32[72]{0:T(128)} %select_reduce_fusion.code_ref, bf16[2,16,3,4,32,128]{5,4,3,2,1,0:T(8,128)(2,1)} %get-tuple-element.45.x_ref.rest_3_, bf16[72,2,16,16,128]{4,3,2,1,0:T(8,128)(2,1)} %k_ref.5, bf16[72,2,16,16,128]{4,3,2,1,0:T(8,128)(2,1)} %v_ref.5), custom_call_target="tpu_custom_call" | custom-call | flops 1000000000 | bytes 9437184 | tf_op jit(solution)/shard_map/attend_pages/pallas_call | solution.py:318
  361.0 8.5 %merge_chip.3.refs_0_ = f32[16,5,32,128]{3,2,1,0:T(8,128)} custom-call(f32[2,16,5,32,128]{4,3,2,1,0:T(8,128)} %attend_pages.3.acc_ref), custom_call_target="tpu_custom_call" | custom-call | flops 1000000000 | bytes 8388608 | tf_op jit(solution)/shard_map/merge_chip/pallas_call | solution.py:482
  369.6 0.7 subtract_bitcast_fusion.1
  370.3 0.1 select_reduce_fusion.3
  370.4 0.6 compare_select_fusion.offset_ref
  371.0 0.6 compare_select_fusion.2.first_ref
  371.6 5.1 %place_pages.2 = (bf16[72,2,16,16,128]{4,3,2,1,0:T(8,128)(2,1)}, bf16[72,2,16,16,128]{4,3,2,1,0:T(8,128)(2,1)}) custom-call(s32[72]{0:T(128)} %select_reduce_fusion.2.from_ref, s32[72]{0:T(128)} %compare_select_fusion.2.first_ref, s32[72]{0:T(128)} %copy-done.3, s32[128]{0:T(128)} %compare_select_fusion.offset_ref, ...), custom_call_target="tpu_custom_call", output_to_operand_aliasing={{0}: (7, {}), {1}: (8, {})} | custom-call | flops 600000000 | bytes 12582912 | tf_op jit(solution)/shard_map/place_pages/pallas_call | solution.py:241
  376.7 100.7 %end_layer.3 = (bf16[8,2048]{1,0:T(8,128)(2,1)}, bf16[32,1,2,16,16,128]{5,4,3,2,1,0:T(8,128)(2,1)}) custom-call(f32[16,5,32,128]{3,2,1,0:T(8,128)} %merge_chip.3.refs_0_, bf16[3,4,32,128]{3,2,1,0:T(8,128)(2,1)} %get-tuple-element.53.refs_1_, bf16[8,2048]{1,0:T(8,128)(2,1)} %get-tuple-element.54.refs_2_, ...), custom_call_target="tpu_custom_call" | custom-call | flops 10000000000 | bytes 134217728 | tf_op jit(solution)/shard_map/end_layer/pallas_call | solution.py:729
  477.5 0.8 reshape.73
  478.3 0.7 bitcast_select_fusion
  479.0 0.0 all-to-all-done.2.rest_0_
  479.0 10.0 %place_pages.3 = (bf16[72,2,16,16,128]{4,3,2,1,0:T(8,128)(2,1)}, bf16[72,2,16,16,128]{4,3,2,1,0:T(8,128)(2,1)}) custom-call(s32[72]{0:T(128)} %select_reduce_fusion.2.from_ref, s32[72]{0:T(128)} %compare_select_fusion.2.first_ref, s32[72]{0:T(128)} %copy-done.3, s32[128]{0:T(128)} %compare_select_fusion.offset_ref, ...), custom_call_target="tpu_custom_call", output_to_operand_aliasing={{0}: (8, {}), {1}: (9, {})} | custom-call | flops 400000000 | bytes 8388608 | tf_op jit(solution)/shard_map/place_pages/pallas_call | solution.py:241
  (17 shorter events, 0.2 us)
Async XLA Ops:
  8.5 8.8 %copy-start.1 = (bf16[2,4,2048]{2,1,0:T(4,128)(2,1)S(1)}, bf16[2,4,2048]{2,1,0:T(4,128)(2,1)}, u32[]{:S(2)}) copy-start(bf16[2,4,2048]{2,1,0:T(4,128)(2,1)} %param.15) | copy-start | bytes 98308
  8.5 87.9 %all-to-all-start = ((bf16[32,1,2,16,16,128]{5,4,3,2,1,0:T(8,128)(2,1)}), bf16[32,1,2,16,16,128]{5,4,3,2,1,0:T(8,128)(2,1)}, u32[]{:S(2)}, u32[]{:S(2)}) async-start(bf16[32,1,2,16,16,128]{5,4,3,2,1,0:T(8,128)(2,1)} %pack_pages.2), calls=%async_computation | async-start | bytes 8388608 | tf_op jit(solution)/shard_map/all_to_all | solution.py:787
  17.4 9.2 %copy-start = (bf16[8,2048]{1,0:T(8,128)(2,1)}, bf16[8,2048]{1,0:T(8,128)(2,1)S(1)}, u32[]{:S(2)}) copy-start(bf16[8,2048]{1,0:T(8,128)(2,1)S(1)} %reshape.72.refs_2_) | copy-start | bytes 98308
  61.8 39.1 %copy-start.4 = (s32[128,12]{0,1:T(8,128)S(1)}, s32[128,12]{0,1:T(8,128)}, u32[]{:S(2)}) copy-start(s32[128,12]{0,1:T(8,128)} %param.24) | copy-start | bytes 18436
  61.8 39.3 %copy-start.5 = (s32[128]{0:T(128)S(1)}, s32[128]{0:T(128)}, u32[]{:S(2)}) copy-start(s32[128]{0:T(128)} %param.26) | copy-start | bytes 1540
  96.4 246.3 %all-to-all-start.1 = ((bf16[32,1,2,16,16,128]{5,4,3,2,1,0:T(8,128)(2,1)}), bf16[32,1,2,16,16,128]{5,4,3,2,1,0:T(8,128)(2,1)}, u32[]{:S(2)}, u32[]{:S(2)}) async-start(bf16[32,1,2,16,16,128]{5,4,3,2,1,0:T(8,128)(2,1)} %get-tuple-element.46), calls=%async_computation.1 | async-start | bytes 8388608 | tf_op jit(solution)/shard_map/all_to_all | solution.py:787
  342.7 4.1 copy-start.6
  342.7 136.2 %all-to-all-start.2 = ((bf16[32,1,2,16,16,128]{5,4,3,2,1,0:T(8,128)(2,1)}), bf16[32,1,2,16,16,128]{5,4,3,2,1,0:T(8,128)(2,1)}, u32[]{:S(2)}, u32[]{:S(2)}) async-start(bf16[32,1,2,16,16,128]{5,4,3,2,1,0:T(8,128)(2,1)} %get-tuple-element.57), calls=%async_computation.2 | async-start | bytes 8388608 | tf_op jit(solution)/shard_map/all_to_all | solution.py:787
  346.9 24.1 %copy-start.2 = (s32[72]{0:T(128)S(1)}, s32[72]{0:T(128)}, u32[]{:S(2)}) copy-start(s32[72]{0:T(128)} %select_reduce_fusion.2.from_ref) | copy-start | bytes 868
  370.4 1.2 copy-start.3

commit v2 on v1

--- a/solution.py
+++ b/solution.py
@@ -12,6 +12,35 @@
 VMEM = pl.BlockSpec(memory_space=pltpu.VMEM)
 SMEM = pl.BlockSpec(memory_space=pltpu.SMEM)
 LOW = -1e30
+
+
+def chip_offsets(chips):
+    side = 1
+    while side * side < chips:
+        side += 1
+    if side * side != chips:
+        return [(j, 0) for j in range(1, chips)], chips
+
+    def near(d):
+        d %= side
+        return d if 2 * d <= side else d - side
+
+    def cost(offset):
+        x, y = near(offset[0]), near(offset[1])
+        return (x == 0 or y == 0, 2 * abs(x) == side or 2 * abs(y) == side, x == 0, abs(x) + abs(y), abs(x), abs(y), x * y < 0, x)
+
+    every = [(x, y) for x in range(side) for y in range(side) if x or y]
+    return sorted(every, key=cost), side
+
+
+def chip_at(chip, offset, side, chips):
+    x, y = offset
+    return lax.rem(chip // side + y, chips // side) * side + lax.rem(lax.rem(chip, side) + x, side)
+
+
+def chip_from(chip, offset, side, chips):
+    x, y = offset
+    return chip_at(chip, ((side - x) % side, (chips // side - y) % (chips // side)), side, chips)
 
 
 def ring(count, depth, lead, start_in, wait_in, start_out, wait_out):
@@ -136,52 +165,14 @@
     )(from_page, k_pool, v_pool)
 
 
-def place_kernel(depth, lead, plan, patches, seq_dev, n_rows, from_ref, first_ref, second_ref, offset_ref, *rest):
+def place_kernel(depth, lead, plan, from_ref, *rest):
     arrived, rest = rest[:len(plan)], rest[len(plan):]
-    rows = rest[:n_rows]
-    k_out, v_out, buf, listed, sems_in, sems_out, staged, entries, sem_row = rest[n_rows + 2:]
+    k_out, v_out, buf, listed, sems_in, sems_out = rest[2:]
     pools = (k_out, v_out)
     peers = arrived[0].shape[0]
-    slots, n_batch = from_ref.shape[0], offset_ref.shape[0]
-    heads = k_out.shape[3]
-
-    def came(slot, r):
-        return (from_ref[slot] >= r * peers) & (from_ref[slot] < (r + 1) * peers)
-
-    def fetch(at, seq, step, h):
-        home, place = seq // seq_dev, lax.rem(seq, seq_dev)
-        return [
-            pltpu.make_async_copy(
-                x.at[lax.rem(home, 2), home // 2, 1 + h, place, pl.ds(step * heads, heads)], staged.at[at, layer], sem_row.at[0]
-            )
-            for layer, x in enumerate(rows)
-        ]
-
-    ends = []
-    found = jnp.int32(0)
-    for h, rounds, inside in patches:
-        def collect(slot, count):
-            hit = jnp.bool_(False)
-            for r in rounds:
-                hit = hit | came(slot, r)
-            for step, ref in enumerate((first_ref, second_ref)):
-                seq = ref[slot]
-                take = (seq >= 0) & (hit == inside)
-
-                @pl.when(take)
-                def _():
-                    entries[count] = (slot * 2 + step) * n_batch + seq
-                    for c in fetch(count, seq, step, h):
-                        c.start()
-
-                count = count + take.astype(jnp.int32)
-            return count
-
-        found = lax.fori_loop(0, slots, collect, found)
-        ends.append(found)
-
+    slots = from_ref.shape[0]
     for part, (r, halves) in enumerate(plan):
-        count = compact(slots, lambda i: came(i, r), lambda i: i, listed)
+        count = compact(slots, lambda i: (from_ref[i] >= r * peers) & (from_ref[i] < (r + 1) * peers), lambda i: i, listed)
 
         def ins(i):
             at = lax.rem(i, depth)
@@ -200,62 +191,154 @@
             lambda i: [c.wait() for c in outs(i)],
         )
 
-    if patches:
-        def fetched(i, carry):
-            for c in fetch(i, 0, 0, 0):
-                c.wait()
-            return carry
-
-        lax.fori_loop(0, found, fetched, 0)
-        begin = jnp.int32(0)
-        for (h, _, _), end in zip(patches, ends):
-            def row_outs(i):
-                entry = entries[i]
-                seq, at = lax.rem(entry, n_batch), entry // n_batch
-                slot, step = at // 2, lax.rem(at, 2)
-                return [
-                    pltpu.make_async_copy(staged.at[i, layer], pools[h].at[slot, layer, offset_ref[seq] + step], sem_row.at[1])
-                    for layer in range(n_rows)
-                ]
-
-            def start(i, carry):
-                for c in row_outs(i):
-                    c.start()
-                return carry
-
-            lax.fori_loop(begin, end, start, 0)
-            begin = end
-
-        def written(i, carry):
-            for layer in range(n_rows):
-                pltpu.make_async_copy(staged.at[i, layer], k_out.at[0, layer, 0], sem_row.at[1]).wait()
-            return carry
-
-        lax.fori_loop(0, found, written, 0)
-
-
-def place_pages(plan, patches, seq_dev, from_page, first_seq, second_seq, offsets, arrived, rows, k_out, v_out):
+
+def place_pages(plan, from_page, arrived, k_out, v_out):
     depth, lead = 24, 12
-    first_pool = 4 + len(arrived) + len(rows)
-    most = max(2 * len(patches) * k_out.shape[0], 1)
     return pl.pallas_call(
-        functools.partial(place_kernel, depth, lead, plan, patches, seq_dev, len(rows)),
+        functools.partial(place_kernel, depth, lead, plan),
         out_shape=[jax.ShapeDtypeStruct(k_out.shape, k_out.dtype)] * 2,
-        in_specs=[SMEM] * 4 + [ANY] * (len(arrived) + len(rows) + 2),
+        in_specs=[SMEM] + [ANY] * (len(arrived) + 2),
         out_specs=[ANY] * 2,
         scratch_shapes=[
             pltpu.VMEM((depth, 2) + k_out.shape[1:], k_out.dtype),
             pltpu.SMEM((k_out.shape[0],), jnp.int32),
             pltpu.SemaphoreType.DMA((depth, 2)),
             pltpu.SemaphoreType.DMA((depth, 2)),
-            pltpu.VMEM((most, max(len(rows), 1)) + k_out.shape[3:], k_out.dtype),
-            pltpu.SMEM((most,), jnp.int32),
+        ],
+        input_output_aliases={1 + len(arrived): 0, 2 + len(arrived): 1},
+        cost_estimate=pl.CostEstimate(flops=2 * 10 ** 8 * len(arrived), bytes_accessed=2 ** 22 * len(arrived), transcendentals=0),
+        name="place_pages",
+    )(from_page, *arrived, k_out, v_out)
+
+
+def close_kernel(seq_dev, first_line, n_rows, from_ref, first_ref, second_ref, offset_ref, k_came, v_came, *rest):
+    rows = rest[:n_rows]
+    k_out, v_out, buf, listed, staged, early, late, sems_in, sem_out, sem_row = rest[n_rows + 2:]
+    pools, arrived = (k_out, v_out), (k_came, v_came)
+    peers = k_came.shape[0]
+    slots, n_batch = from_ref.shape[0], offset_ref.shape[0]
+    heads = k_out.shape[3]
+    most = early.shape[0]
+
+    def ins(i, line):
+        return [pltpu.make_async_copy(ref.at[line], buf.at[i, h], sems_in.at[i]) for h, ref in enumerate(arrived)]
+
+    def outs(i, slot):
+        return [pltpu.make_async_copy(buf.at[i, h], pools[h].at[slot], sem_out.at[0]) for h in range(2)]
+
+    def fetch(at, seq, step):
+        home, place = seq // seq_dev, lax.rem(seq, seq_dev)
+        return [
+            pltpu.make_async_copy(
+                x.at[lax.rem(home, 2), home // 2, 1 + h, place, pl.ds(step * heads, heads)], staged.at[at, layer, h], sem_row.at[0]
+            )
+            for layer, x in enumerate(rows) for h in range(2)
+        ]
+
+    def write(at, slot, layer_offset, sem):
+        return [
+            pltpu.make_async_copy(staged.at[at, layer, h], pools[h].at[slot, layer, layer_offset], sem_row.at[sem])
+            for layer in range(n_rows) for h in range(2)
+        ]
+
+    def scan(slot, counts):
+        pages, n_early, n_late = counts
+        line = from_ref[slot] - first_line
+        moved = (line >= 0) & (line < peers)
+
+        @pl.when(moved)
+        def _():
+            listed[pages] = slot
+            for c in ins(pages, line):
+                c.start()
+
+        for step, ref in enumerate((first_ref, second_ref)):
+            seq = ref[slot]
+            entry = (slot * 2 + step) * n_batch + seq
+
+            @pl.when((seq >= 0) & moved)
+            def _():
+                late[n_late] = entry
+                for c in fetch(most - 1 - n_late, seq, step):
+                    c.start()
+
+            @pl.when((seq >= 0) & jnp.logical_not(moved))
+            def _():
+                early[n_early] = entry
+                for c in fetch(n_early, seq, step):
+                    c.start()
+
+            n_late = n_late + ((seq >= 0) & moved).astype(jnp.int32)
+            n_early = n_early + ((seq >= 0) & jnp.logical_not(moved)).astype(jnp.int32)
+        return pages + moved.astype(jnp.int32), n_early, n_late
+
+    pages, n_early, n_late = lax.fori_loop(0, slots, scan, (jnp.int32(0), jnp.int32(0), jnp.int32(0)))
+
+    def pass_on(i, carry):
+        for c in ins(i, 0):
+            c.wait()
+        for c in outs(i, listed[i]):
+            c.start()
+        return carry
+
+    lax.fori_loop(0, pages, pass_on, 0)
+
+    def fetched(i, carry):
+        for c in fetch(0, 0, 0):
+            c.wait()
+        return carry
+
+    lax.fori_loop(0, n_early + n_late, fetched, 0)
+
+    def write_row(entries, at, sem):
+        def body(i, carry):
+            entry = entries[i]
+            seq, where = lax.rem(entry, n_batch), entry // n_batch
+            for c in write(at(i), where // 2, offset_ref[seq] + lax.rem(where, 2), sem):
+                c.start()
+            return carry
+        return body
+
+    lax.fori_loop(0, n_early, write_row(early, lambda i: i, 1), 0)
+
+    def placed(i, carry):
+        for c in outs(i, 0):
+            c.wait()
+        return carry
+
+    lax.fori_loop(0, pages, placed, 0)
+    lax.fori_loop(0, n_late, write_row(late, lambda i: most - 1 - i, 1), 0)
+
+    def written(i, carry):
+        for c in write(0, 0, 0, 1):
+            c.wait()
+        return carry
+
+    lax.fori_loop(0, n_early + n_late, written, 0)
+
+
+def close_pools(seq_dev, last_round, from_page, first_seq, second_seq, offsets, arrived, rows, k_out, v_out):
+    peers, slots = arrived[0].shape[0], k_out.shape[0]
+    first_pool = 6 + len(rows)
+    return pl.pallas_call(
+        functools.partial(close_kernel, seq_dev, last_round * peers, len(rows)),
+        out_shape=[jax.ShapeDtypeStruct(k_out.shape, k_out.dtype)] * 2,
+        in_specs=[SMEM] * 4 + [ANY] * (4 + len(rows)),
+        out_specs=[ANY] * 2,
+        scratch_shapes=[
+            pltpu.VMEM((peers, 2) + k_out.shape[1:], k_out.dtype),
+            pltpu.SMEM((peers,), jnp.int32),
+            pltpu.VMEM((2 * slots, len(rows), 2) + k_out.shape[3:], k_out.dtype),
+            pltpu.SMEM((2 * slots,), jnp.int32),
+            pltpu.SMEM((2 * slots,), jnp.int32),
+            pltpu.SemaphoreType.DMA((peers,)),
+            pltpu.SemaphoreType.DMA((1,)),
             pltpu.SemaphoreType.DMA((2,)),
         ],
         input_output_aliases={first_pool: 0, first_pool + 1: 1},
-        cost_estimate=pl.CostEstimate(flops=2 * 10 ** 8 * len(arrived), bytes_accessed=2 ** 22 * len(arrived), transcendentals=0),
-        name="place_pages",
-    )(from_page, first_seq, second_seq, offsets, *arrived, *rows, k_out, v_out)
+        cost_estimate=pl.CostEstimate(flops=4 * 10 ** 8, bytes_accessed=2 ** 23, transcendentals=0),
+        name="close_pools",
+    )(from_page, first_seq, second_seq, offsets, *[a.reshape((peers,) + a.shape[2:]) for a in arrived], *rows, k_out, v_out)
 
 
 def attend_kernel(block, pages_seq, seq_dev, page_size, scale, code_ref, x_ref, k_ref, v_ref, acc_ref):
@@ -367,27 +450,23 @@
             device_id={"kv": other}, device_id_type=MESH,
         )
 
-    def start(j, carry):
-        send(j).start()
-        return carry
-
-    lax.fori_loop(1, chips, start, 0)
+    offsets, side = chip_offsets(chips)
+    for offset in offsets:
+        send(lax.rem(chip_at(chip, offset, side, chips) + chips - chip, chips)).start()
     own = forward(x_ref, chip)
     own.start()
     mine = pltpu.make_async_copy(x_ref, out_ref.at[core, chip], copy_sem.at[0])
     mine.start()
 
-    def arrive(j, carry):
-        at = lax.rem(chip + chips - j, chips)
+    for offset in offsets:
+        at = chip_from(chip, offset, side, chips)
+        j = lax.rem(chip + chips - at, chips)
         pltpu.make_async_remote_copy(
             src_ref=x_ref, dst_ref=held.at[core, at], send_sem=send_sem.at[j], recv_sem=recv_sem.at[at],
             device_id={"kv": other}, device_id_type=MESH,
         ).wait_recv()
         forward(held.at[core, at], at).start()
         pltpu.make_async_copy(held.at[core, at], out_ref.at[core, at], copy_sem.at[j]).start()
-        return carry
-
-    lax.fori_loop(1, chips, arrive, 0)
 
     def passed(j, carry):
         at = lax.rem(chip + j, chips)
@@ -561,17 +640,14 @@
             device_id={"kv": anyone(j)}, device_id_type=MESH,
         )
 
-    def start(j, carry):
-        send(j).start()
-        return carry
-
-    lax.fori_loop(1, chips, start, 0)
-
-    def start_pages(j, carry):
-        send_pages(j).start()
-        return carry
-
-    lax.fori_loop(1, n, start_pages, 0)
+    offsets, side = chip_offsets(chips)
+    for offset in offsets:
+        send(lax.rem(chip_at(chip, offset, side, chips) + chips - chip, chips)).start()
+    for offset in offsets:
+        for other_core in range(2):
+            to = 2 * chip_at(chip, offset, side, chips) + lax.rem(core + other_core, 2)
+            send_pages(lax.rem(to + n - me, n)).start()
+    send_pages(lax.rem(me + 1 - 2 * core + n - me, n)).start()
     held[chip] = sums_ref[chip]
 
     queries = [x_ref[0, i].astype(jnp.float32) for i in range(seq_dev)]
@@ -794,6 +870,7 @@
 
         plan = ((0, (0,)), (0, (1,))) + tuple((r, (0, 1)) for r in range(1, rounds - 1)) + ((rounds - 1, (0,)), (rounds - 1, (1,)))
         packed = list(pack_pages(plan[:1], send_slot, k_pool, v_pool, groups))
+        packed[0], send_slot = lax.optimization_barrier((packed[0], send_slot))
         got = [exchange(packed[0])]
         packed += list(pack_pages(plan[1:], send_slot, k_pool, v_pool, groups))
         tables = (from_page, first_seq, second_seq, offsets)
@@ -804,7 +881,7 @@
             jnp.dot(hidden, w[0], preferred_element_type=jnp.float32).astype(jnp.bfloat16).reshape(seq_dev, steps * heads, head_dim)
             for w in (w_query, w_key, w_value)
         ])
-        x, k_out, v_out, packed = lax.optimization_barrier((x, k_out, v_out, packed))
+        x, k_out, v_out, packed, got = lax.optimization_barrier((x, k_out, v_out, packed, got))
         x_all = spread(x, groups)
         rows = []
         for layer in range(n_layers):
@@ -812,15 +889,14 @@
             x_all = send_next(x_all, 1)
             sums = merge_chip(attend_pages(code, x_all, k_pool, v_pool, layer, pages_seq))
             if layer:
-                k_out, v_out = place_pages(plan[:3], (), seq_dev, *tables, got[:3], [], k_out, v_out)
+                k_out, v_out = place_pages(plan[:3], from_page, got[:3], k_out, v_out)
                 sums, k_out, v_out = lax.optimization_barrier((sums, k_out, v_out))
             follow = (w_query, w_key, w_value) if layer + 1 < n_layers else ()
             hidden, pages, *ahead = end_layer(sums, x, hidden, packed[len(got)], w_out, w_up, w_down, follow, layer, groups)
             got.append(pages)
             if ahead:
                 x, x_all = ahead
-        everything = ((0, (), False), (1, (), False))
-        k_out, v_out = place_pages(plan[3:], everything, seq_dev, *tables, got[3:], rows, k_out, v_out)
+        k_out, v_out = close_pools(seq_dev, rounds - 1, *tables, got[3:], rows, k_out, v_out)
         hidden = jnp.transpose(hidden.reshape(seq_dev, steps, width), (1, 0, 2))
         done = lax.dynamic_slice(finished, (me * seq_dev,), (seq_dev,)) != 0
         live = jnp.stack([jnp.ones_like(done), ~done])

time: 498 us -> 461 us (0.926); the launches traced: 489 us -> 461 us
  Pallas kernels: 448 us -> 390 us
  waiting for transfers between devices: 0.01 us -> 25.2 us
    pallas_call x2, Pallas kernels: 319 us -> 277 us  [end_layer(): pl.pallas_call(functools.partial(layer_kernel, n, head_dim ** (-0.5), lay...]
    all_to_all x3, waiting for transfers between devices: 0.01 us -> 25.2 us  [exchange(): return lax.all_to_all(block, 'kv', 0, 0, tiled=True)]
    pallas_call x2, Pallas kernels: 19.2 us -> 6.65 us  [pack_pages(): pl.pallas_call(functools.partial(pack_kernel, depth, lead, plan), out_sha...]
    pallas_call x1, Pallas kernels: 15.3 us -> 7.34 us  [keep_pages(): pl.pallas_call(functools.partial(keep_kernel, depth, lead), out_shape=[ja...]
    pallas_call x2, Pallas kernels: 15.1 us -> 22.7 us  [the longest x1 12.5 us: place_pages(): pl.pallas_call(functools.partial(place_kernel, depth, lead, plan), out_sh...]
  transfers between devices with their start and end apart: 3 -> 3, of which waited for: 0 -> 1; matrix products, arithmetic and copies ran while one was open for 4% -> 4% of each run, Pallas kernels for 89% -> 75%
where the time goes in v2:
time: 461 us
  Pallas kernels  390 us (85%)
  waiting for transfers between devices  25.2 us (5%)
  starting transfers between devices  22 us (5%)
  matrix products  13.7 us (3%)
  other arithmetic  8.09 us (2%)
    pallas_call x2, Pallas kernels, end_layer(): pl.pallas_call(functools.partial(layer_kernel, n, head_dim ** (-0.5), lay...  277 us
    pallas_call x1, Pallas kernels, spread(): pl.pallas_call(functools.partial(spread_kernel, n), out_shape=jax.ShapeDt...  31.6 us
    pallas_call x2, Pallas kernels, attend_pages(): pl.pallas_call(functools.partial(attend_kernel, block, pages_seq, seq_dev...  28.2 us
    all_to_all x3, waiting for transfers between devices, exchange(): return lax.all_to_all(block, 'kv', 0, 0, tiled=True)  25.2 us
    all_to_all x3, starting transfers between devices, exchange(): return lax.all_to_all(block, 'kv', 0, 0, tiled=True)  22 us
    pallas_call x2, Pallas kernels, merge_chip(): pl.pallas_call(merge_chip_kernel, out_shape=jax.ShapeDtypeStruct(blocks,...  16.7 us
    dot_general x3, matrix products, device_fn(): jnp.dot(hidden, w[0], preferred_element_type=jnp.float32)  13.7 us
    pallas_call x1, Pallas kernels, place_pages(): pl.pallas_call(functools.partial(place_kernel, depth, lead, plan), out_sh...  12.5 us
  transfers between devices with their start and end apart: 3, of which 1 were waited for; matrix products, arithmetic and copies ran while one was open for 4% of the time, Pallas kernels for 75%

profile of v2, /device:TPU:97, one launch (start us, length us, event | category | flops | bytes accessed | tf_op | source)
XLA Modules:
  0.0 461.5 jit_solution(6711564010697391095)
XLA Ops:
  0.6 0.7 broadcast_compare_fusion
  1.3 0.7 multiply_add_fusion.1
  2.1 0.4 convert_reduce_fusion
  2.4 0.7 multiply_add_fusion.2
  3.1 0.7 select_reduce_fusion.1.slot_ref
  3.8 2.2 pack_pages.2
  6.0 0.0 copy-start.1
  6.1 11.3 %all-to-all-start = ((bf16[32,1,2,16,16,128]{5,4,3,2,1,0:T(8,128)(2,1)}), bf16[32,1,2,16,16,128]{5,4,3,2,1,0:T(8,128)(2,1)}, u32[]{:S(2)}, u32[]{:S(2)}) async-start(bf16[32,1,2,16,16,128]{5,4,3,2,1,0:T(8,128)(2,1)} %pack_pages.2), calls=%async_computation | async-start | bytes 8388608 | tf_op jit(solution)/shard_map/all_to_all | solution.py:863
  17.3 0.0 copy-done.1
  17.4 0.0 copy-start
  17.4 4.6 fusion.13
  22.1 4.6 fusion.16
  26.7 4.6 fusion.10
  31.3 4.4 pack_pages.3
  35.7 0.7 select_reduce_fusion.2.from_ref
  36.4 7.3 %keep_pages.1 = (bf16[72,2,16,16,128]{4,3,2,1,0:T(8,128)(2,1)}, bf16[72,2,16,16,128]{4,3,2,1,0:T(8,128)(2,1)}) custom-call(s32[72]{0:T(128)} %select_reduce_fusion.2.from_ref, bf16[72,2,16,16,128]{4,3,2,1,0:T(8,128)(2,1)} %k_ref.5, bf16[72,2,16,16,128]{4,3,2,1,0:T(8,128)(2,1)} %v_ref.5), custom_call_target="tpu_custom_call" | custom-call | flops 1000000000 | bytes 33554432 | tf_op jit(solution)/shard_map/keep_pages/pallas_call | solution.py:152
  43.7 0.0 copy-start.3
  43.7 0.0 copy-start.5
  43.8 0.7 pad_maximum_fusion.x_ref.refs_1_
  44.4 25.2 %all-to-all-done.rest_0_ = bf16[32,1,2,16,16,128]{5,4,3,2,1,0:T(8,128)(2,1)} async-done(((bf16[32,1,2,16,16,128]{5,4,3,2,1,0:T(8,128)(2,1)}), bf16[32,1,2,16,16,128]{5,4,3,2,1,0:T(8,128)(2,1)}, u32[]{:S(2)}, u32[]{:S(2)}) %all-to-all-start) | async-done | bytes 4194336 | tf_op jit(solution)/shard_map/all_to_all | solution.py:863
  69.6 31.6 %spread_queries.1.x_ref.rest_0_ = bf16[2,16,3,4,32,128]{5,4,3,2,1,0:T(8,128)(2,1)} custom-call(bf16[3,4,32,128]{3,2,1,0:T(8,128)(2,1)} %pad_maximum_fusion.x_ref.refs_1_), custom_call_target="tpu_custom_call" | custom-call | tf_op jit(solution)/shard_map/spread_queries/pallas_call | solution.py:504
  101.2 4.0 all-to-all-start.1
  105.2 0.1 copy.32
  105.4 0.1 sub.78
  105.5 0.0 copy-done.5
  105.5 0.1 subtract_clamp_fusion
  105.6 0.1 min.12
  105.7 0.7 select_reduce_fusion.code_ref
  106.4 14.1 %attend_pages.2.acc_ref = f32[2,16,5,32,128]{4,3,2,1,0:T(8,128)} custom-call(s32[72]{0:T(128)} %select_reduce_fusion.code_ref, bf16[2,16,3,4,32,128]{5,4,3,2,1,0:T(8,128)(2,1)} %spread_queries.1.x_ref.rest_0_, bf16[72,2,16,16,128]{4,3,2,1,0:T(8,128)(2,1)} %k_ref.5, bf16[72,2,16,16,128]{4,3,2,1,0:T(8,128)(2,1)} %v_ref.5), custom_call_target="tpu_custom_call" | custom-call | flops 1000000000 | bytes 9437184 | tf_op jit(solution)/shard_map/attend_pages/pallas_call | solution.py:401
  120.5 8.2 %merge_chip.2.refs_0_ = f32[16,5,32,128]{3,2,1,0:T(8,128)} custom-call(f32[2,16,5,32,128]{4,3,2,1,0:T(8,128)} %attend_pages.2.acc_ref), custom_call_target="tpu_custom_call" | custom-call | flops 1000000000 | bytes 8388608 | tf_op jit(solution)/shard_map/merge_chip/pallas_call | solution.py:561
  128.8 178.0 %end_layer.2 = (bf16[8,2048]{1,0:T(8,128)(2,1)}, bf16[32,2,2,16,16,128]{5,4,3,2,1,0:T(8,128)(2,1)}, bf16[3,4,32,128]{3,2,1,0:T(8,128)(2,1)}, bf16[2,16,3,4,32,128]{5,4,3,2,1,0:T(8,128)(2,1)}) custom-call(f32[16,5,32,128]{3,2,1,0:T(8,128)} %merge_chip.2.refs_0_, bf16[3,4,32,128]{3,2,1,0:T(8,128)(2,1)} %pad_maximum_fusion.x_ref.refs_1_, ...), custom_call_target="tpu_custom_call" | custom-call | flops 10000000000 | bytes 134217728 | tf_op jit(solution)/shard_map/end_layer/pallas_call | solution.py:805
  306.8 0.0 copy-start.6
  306.8 0.0 all-to-all-done.1.rest_1_
  306.8 6.8 %all-to-all-start.2 = ((bf16[32,1,2,16,16,128]{5,4,3,2,1,0:T(8,128)(2,1)}), bf16[32,1,2,16,16,128]{5,4,3,2,1,0:T(8,128)(2,1)}, u32[]{:S(2)}, u32[]{:S(2)}) async-start(bf16[32,1,2,16,16,128]{5,4,3,2,1,0:T(8,128)(2,1)} %get-tuple-element.63), calls=%async_computation.2 | async-start | bytes 8388608 | tf_op jit(solution)/shard_map/all_to_all | solution.py:863
  313.6 0.1 not_bitcast_fusion
  313.7 0.7 subtract_bitcast_fusion.1
  314.4 0.1 select_reduce_fusion.3
  314.5 0.0 copy-start.4
  314.5 0.6 compare_select_fusion.offset_ref
  315.1 0.6 compare_select_fusion.2.first_ref
  315.7 14.1 %attend_pages.3.acc_ref = f32[2,16,5,32,128]{4,3,2,1,0:T(8,128)} custom-call(s32[72]{0:T(128)} %select_reduce_fusion.code_ref, bf16[2,16,3,4,32,128]{5,4,3,2,1,0:T(8,128)(2,1)} %get-tuple-element.50.x_ref.rest_1_, bf16[72,2,16,16,128]{4,3,2,1,0:T(8,128)(2,1)} %k_ref.5, bf16[72,2,16,16,128]{4,3,2,1,0:T(8,128)(2,1)} %v_ref.5), custom_call_target="tpu_custom_call" | custom-call | flops 1000000000 | bytes 9437184 | tf_op jit(solution)/shard_map/attend_pages/pallas_call | solution.py:401
  329.8 8.5 %merge_chip.3.refs_0_ = f32[16,5,32,128]{3,2,1,0:T(8,128)} custom-call(f32[2,16,5,32,128]{4,3,2,1,0:T(8,128)} %attend_pages.3.acc_ref), custom_call_target="tpu_custom_call" | custom-call | flops 1000000000 | bytes 8388608 | tf_op jit(solution)/shard_map/merge_chip/pallas_call | solution.py:561
  338.3 12.5 %place_pages.1 = (bf16[72,2,16,16,128]{4,3,2,1,0:T(8,128)(2,1)}, bf16[72,2,16,16,128]{4,3,2,1,0:T(8,128)(2,1)}) custom-call(s32[72]{0:T(128)} %select_reduce_fusion.2.from_ref, bf16[32,1,2,16,16,128]{5,4,3,2,1,0:T(8,128)(2,1)} %all-to-all-done.rest_0_, ...), custom_call_target="tpu_custom_call", output_to_operand_aliasing={{0}: (4, {}), {1}: (5, {})} | custom-call | flops 600000000 | bytes 12582912 | tf_op jit(solution)/shard_map/place_pages/pallas_call | solution.py:197
  350.8 98.8 %end_layer.3 = (bf16[8,2048]{1,0:T(8,128)(2,1)}, bf16[32,1,2,16,16,128]{5,4,3,2,1,0:T(8,128)(2,1)}) custom-call(f32[16,5,32,128]{3,2,1,0:T(8,128)} %merge_chip.3.refs_0_, bf16[3,4,32,128]{3,2,1,0:T(8,128)(2,1)} %get-tuple-element.59.refs_1_, bf16[8,2048]{1,0:T(8,128)(2,1)} %get-tuple-element.60.refs_2_, ...), custom_call_target="tpu_custom_call" | custom-call | flops 10000000000 | bytes 134217728 | tf_op jit(solution)/shard_map/end_layer/pallas_call | solution.py:805
  449.6 0.8 reshape.79
  450.4 0.7 bitcast_select_fusion
  451.1 0.0 all-to-all-done.2
  451.1 10.2 %close_pools.1 = (bf16[72,2,16,16,128]{4,3,2,1,0:T(8,128)(2,1)}, bf16[72,2,16,16,128]{4,3,2,1,0:T(8,128)(2,1)}) custom-call(s32[72]{0:T(128)} %select_reduce_fusion.2.from_ref, s32[72]{0:T(128)} %compare_select_fusion.2.first_ref, s32[72]{0:T(128)} %copy-done.4, s32[128]{0:T(128)} %compare_select_fusion.offset_ref, ...), custom_call_target="tpu_custom_call", output_to_operand_aliasing={{0}: (8, {}), {1}: (9, {})} | custom-call | flops 400000000 | bytes 8388608 | tf_op jit(solution)/shard_map/close_pools/pallas_call | solution.py:323
  (17 shorter events, 0.2 us)
Async XLA Ops:
  6.0 11.3 %copy-start.1 = (bf16[2,4,2048]{2,1,0:T(4,128)(2,1)S(1)}, bf16[2,4,2048]{2,1,0:T(4,128)(2,1)}, u32[]{:S(2)}) copy-start(bf16[2,4,2048]{2,1,0:T(4,128)(2,1)} %param.15) | copy-start | bytes 98308
  6.1 63.6 %all-to-all-start = ((bf16[32,1,2,16,16,128]{5,4,3,2,1,0:T(8,128)(2,1)}), bf16[32,1,2,16,16,128]{5,4,3,2,1,0:T(8,128)(2,1)}, u32[]{:S(2)}, u32[]{:S(2)}) async-start(bf16[32,1,2,16,16,128]{5,4,3,2,1,0:T(8,128)(2,1)} %pack_pages.2), calls=%async_computation | async-start | bytes 8388608 | tf_op jit(solution)/shard_map/all_to_all | solution.py:863
  17.4 9.2 %copy-start = (bf16[8,2048]{1,0:T(8,128)(2,1)}, bf16[8,2048]{1,0:T(8,128)(2,1)S(1)}, u32[]{:S(2)}) copy-start(bf16[8,2048]{1,0:T(8,128)(2,1)S(1)} %reshape.78.refs_2_) | copy-start | bytes 98308
  43.7 61.5 %copy-start.3 = (s32[128,12]{0,1:T(8,128)S(1)}, s32[128,12]{0,1:T(8,128)}, u32[]{:S(2)}) copy-start(s32[128,12]{0,1:T(8,128)} %param.24) | copy-start | bytes 18436
  43.7 61.7 %copy-start.5 = (s32[128]{0:T(128)S(1)}, s32[128]{0:T(128)}, u32[]{:S(2)}) copy-start(s32[128]{0:T(128)} %param.26) | copy-start | bytes 1540
  101.2 205.6 %all-to-all-start.1 = ((bf16[32,1,2,16,16,128]{5,4,3,2,1,0:T(8,128)(2,1)}), bf16[32,1,2,16,16,128]{5,4,3,2,1,0:T(8,128)(2,1)}, u32[]{:S(2)}, u32[]{:S(2)}) async-start(bf16[32,1,2,16,16,128]{5,4,3,2,1,0:T(8,128)(2,1)} %get-tuple-element.52), calls=%async_computation.1 | async-start | bytes 8388608 | tf_op jit(solution)/shard_map/all_to_all | solution.py:863
  306.8 6.8 %copy-start.6 = (s32[128]{0:T(128)S(1)}, s32[128]{0:T(128)}, u32[]{:S(2)}) copy-start(s32[128]{0:T(128)} %param.27) | copy-start | bytes 1540
  306.8 8.4 %copy-start.2 = (s32[72]{0:T(128)S(1)}, s32[72]{0:T(128)}, u32[]{:S(2)}) copy-start(s32[72]{0:T(128)} %select_reduce_fusion.2.from_ref) | copy-start | bytes 868
  306.8 144.3 %all-to-all-start.2 = ((bf16[32,1,2,16,16,128]{5,4,3,2,1,0:T(8,128)(2,1)}), bf16[32,1,2,16,16,128]{5,4,3,2,1,0:T(8,128)(2,1)}, u32[]{:S(2)}, u32[]{:S(2)}) async-start(bf16[32,1,2,16,16,128]{5,4,3,2,1,0:T(8,128)(2,1)} %get-tuple-element.63), calls=%async_computation.2 | async-start | bytes 8388608 | tf_op jit(solution)/shard_map/all_to_all | solution.py:863
  314.5 15.3 %copy-start.4 = (s32[72]{0:T(128)}, s32[72]{0:T(128)S(1)}, u32[]{:S(2)}) copy-start(s32[72]{0:T(128)S(1)} %get-tuple-element.74.second_ref) | copy-start | bytes 868

commit v3 on v2

--- a/solution.py
+++ b/solution.py
@@ -122,7 +122,7 @@
             pltpu.SemaphoreType.DMA((depth, 2)),
             pltpu.SemaphoreType.DMA((depth, 2)),
         ],
-        cost_estimate=pl.CostEstimate(flops=10 ** 8 * total, bytes_accessed=2 ** 21 * total, transcendentals=0),
+        cost_estimate=pl.CostEstimate(flops=10 ** 6, bytes_accessed=2 ** 21 * total, transcendentals=0),
         name="pack_pages",
     )(send_slot, k_pool, v_pool)
 
@@ -160,7 +160,7 @@
             pltpu.SemaphoreType.DMA((depth, 2)),
             pltpu.SemaphoreType.DMA((depth, 2)),
         ],
-        cost_estimate=pl.CostEstimate(flops=10 ** 9, bytes_accessed=2 ** 25, transcendentals=0),
+        cost_estimate=pl.CostEstimate(flops=10 ** 6, bytes_accessed=2 ** 25, transcendentals=0),
         name="keep_pages",
     )(from_page, k_pool, v_pool)
 
@@ -206,14 +206,14 @@
             pltpu.SemaphoreType.DMA((depth, 2)),
         ],
         input_output_aliases={1 + len(arrived): 0, 2 + len(arrived): 1},
-        cost_estimate=pl.CostEstimate(flops=2 * 10 ** 8 * len(arrived), bytes_accessed=2 ** 22 * len(arrived), transcendentals=0),
+        cost_estimate=pl.CostEstimate(flops=10 ** 6, bytes_accessed=2 ** 22 * len(arrived), transcendentals=0),
         name="place_pages",
     )(from_page, *arrived, k_out, v_out)
 
 
-def close_kernel(seq_dev, first_line, n_rows, from_ref, first_ref, second_ref, offset_ref, k_came, v_came, *rest):
-    rows = rest[:n_rows]
-    k_out, v_out, buf, listed, staged, early, late, sems_in, sem_out, sem_row = rest[n_rows + 2:]
+def close_kernel(seq_dev, first_line, n_layers, from_ref, first_ref, second_ref, offset_ref, k_came, v_came, *rest):
+    rows = rest[:2 * n_layers]
+    k_out, v_out, buf, listed, staged, early, late, sems_in, sem_out, sem_row = rest[2 * n_layers + 2:]
     pools, arrived = (k_out, v_out), (k_came, v_came)
     peers = k_came.shape[0]
     slots, n_batch = from_ref.shape[0], offset_ref.shape[0]
@@ -230,15 +230,15 @@
         home, place = seq // seq_dev, lax.rem(seq, seq_dev)
         return [
             pltpu.make_async_copy(
-                x.at[lax.rem(home, 2), home // 2, 1 + h, place, pl.ds(step * heads, heads)], staged.at[at, layer, h], sem_row.at[0]
+                rows[2 * layer + h].at[lax.rem(home, 2), home // 2, place, pl.ds(step * heads, heads)], staged.at[at, layer, h], sem_row.at[0]
             )
-            for layer, x in enumerate(rows) for h in range(2)
+            for layer in range(n_layers) for h in range(2)
         ]
 
     def write(at, slot, layer_offset, sem):
         return [
             pltpu.make_async_copy(staged.at[at, layer, h], pools[h].at[slot, layer, layer_offset], sem_row.at[sem])
-            for layer in range(n_rows) for h in range(2)
+            for layer in range(n_layers) for h in range(2)
         ]
 
     def scan(slot, counts):
@@ -321,14 +321,14 @@
     peers, slots = arrived[0].shape[0], k_out.shape[0]
     first_pool = 6 + len(rows)
     return pl.pallas_call(
-        functools.partial(close_kernel, seq_dev, last_round * peers, len(rows)),
+        functools.partial(close_kernel, seq_dev, last_round * peers, len(rows) // 2),
         out_shape=[jax.ShapeDtypeStruct(k_out.shape, k_out.dtype)] * 2,
         in_specs=[SMEM] * 4 + [ANY] * (4 + len(rows)),
         out_specs=[ANY] * 2,
         scratch_shapes=[
             pltpu.VMEM((peers, 2) + k_out.shape[1:], k_out.dtype),
             pltpu.SMEM((peers,), jnp.int32),
-            pltpu.VMEM((2 * slots, len(rows), 2) + k_out.shape[3:], k_out.dtype),
+            pltpu.VMEM((2 * slots, len(rows) // 2, 2) + k_out.shape[3:], k_out.dtype),
             pltpu.SMEM((2 * slots,), jnp.int32),
             pltpu.SMEM((2 * slots,), jnp.int32),
             pltpu.SemaphoreType.DMA((peers,)),
@@ -336,13 +336,13 @@
             pltpu.SemaphoreType.DMA((2,)),
         ],
         input_output_aliases={first_pool: 0, first_pool + 1: 1},
-        cost_estimate=pl.CostEstimate(flops=4 * 10 ** 8, bytes_accessed=2 ** 23, transcendentals=0),
+        cost_estimate=pl.CostEstimate(flops=10 ** 6, bytes_accessed=2 ** 23, transcendentals=0),
         name="close_pools",
     )(from_page, first_seq, second_seq, offsets, *[a.reshape((peers,) + a.shape[2:]) for a in arrived], *rows, k_out, v_out)
 
 
-def attend_kernel(block, pages_seq, seq_dev, page_size, scale, code_ref, x_ref, k_ref, v_ref, acc_ref):
-    rows, head_dim = x_ref.shape[-2:]
+def attend_kernel(block, pages_seq, seq_dev, page_size, scale, code_ref, q_ref, k_ref, v_ref, acc_ref):
+    rows, head_dim = q_ref.shape[-2:]
     heads = k_ref.shape[3]
     chips = acc_ref.shape[1]
     step = pl.program_id(0)
@@ -367,7 +367,7 @@
         seq = held // (2 * page_size * pages_seq)
         home, place = seq // seq_dev, lax.rem(seq, seq_dev)
         core, chip = lax.rem(home, 2), home // 2
-        q = x_ref[core, chip, 0, place]
+        q = q_ref[core, chip, place]
         keys = k_ref[s, 0].reshape(page_size * heads, head_dim)
         values = v_ref[s, 0].reshape(page_size * heads, head_dim)
         scores = lax.dot_general(q, keys, (((1,), (1,)), ((), ())), preferred_element_type=jnp.float32) * scale
@@ -391,12 +391,12 @@
         acc_ref[core, chip, seq_dev] = jnp.where(lane == 2 * place, new_top, jnp.where(lane == 2 * place + 1, new_total, stats))
 
 
-def attend_pages(code, x_all, k_pool, v_pool, layer, pages_seq):
+def attend_pages(code, q_all, k_pool, v_pool, layer, pages_seq):
     slots, _, page_size, heads, head_dim = k_pool.shape
-    cores, chips, _, seq_dev, rows, _ = x_all.shape
+    cores, chips, seq_dev, rows, _ = q_all.shape
     block = 8
     page_spec = pl.BlockSpec((block, 1, page_size, heads, head_dim), lambda i, c: (i, layer, 0, 0, 0))
-    query_spec = pl.BlockSpec((cores, chips, 1, seq_dev, rows, head_dim), lambda i, c: (0,) * 6)
+    query_spec = pl.BlockSpec(q_all.shape, lambda i, c: (0,) * 5)
     acc_shape = (cores, chips, seq_dev + 1, rows, head_dim)
     return pl.pallas_call(
         functools.partial(attend_kernel, block, pages_seq, seq_dev, page_size, head_dim ** -0.5),
@@ -408,9 +408,9 @@
             out_specs=pl.BlockSpec(acc_shape, lambda i, c: (0,) * 5),
         ),
         compiler_params=pltpu.CompilerParams(dimension_semantics=("arbitrary",)),
-        cost_estimate=pl.CostEstimate(flops=10 ** 9, bytes_accessed=2 * slots * page_size * heads * head_dim * 2, transcendentals=0),
+        cost_estimate=pl.CostEstimate(flops=10 ** 6, bytes_accessed=2 * slots * page_size * heads * head_dim * 2, transcendentals=0),
         name="attend_pages",
-    )(code, x_all, k_pool, v_pool)
+    )(code, q_all, k_pool, v_pool)
 
 
 def spread_kernel(n, x_ref, out_ref, held, send_sem, recv_sem, pass_sem, got_sem, copy_sem):
@@ -515,7 +515,7 @@
             pltpu.SemaphoreType.DMA((n,)),
         ],
         compiler_params=pltpu.CompilerParams(collective_id=0, has_side_effects=True),
-        name="spread_queries",
+        name="spread_rows",
     )(x)
 
 
@@ -569,7 +569,7 @@
             pltpu.SemaphoreType.DMA((1,)),
         ],
         compiler_params=pltpu.CompilerParams(collective_id=2, has_side_effects=True),
-        cost_estimate=pl.CostEstimate(flops=10 ** 9, bytes_accessed=2 ** 23, transcendentals=0),
+        cost_estimate=pl.CostEstimate(flops=10 ** 6, bytes_accessed=2 ** 23, transcendentals=0),
         name="merge_chip",
     )(acc)
 
@@ -577,13 +577,10 @@
 def layer_kernel(n, scale, layer, follow, *refs):
     sums_ref, x_ref, hid_ref, chunk_ref, wo_ref, wu_ref, wd_ref = refs[:7]
     refs = refs[7:]
-    if follow:
-        proj, refs = refs[:3], refs[3:]
     hid_out, got_ref = refs[:2]
     refs = refs[2:]
     if follow:
-        x_out, all_out = refs[:2]
-        refs = refs[2:]
+        all_out, refs = refs[0], refs[1:]
     held, o_scr, rows_scr, mid_scr, acc_scr, wide, up, down, wide_sem, up_sem, down_sem, send_sem, recv_sem, page_send, page_recv = refs[:15]
     refs = refs[15:]
     me = lax.axis_index("kv")
@@ -593,7 +590,7 @@
     core, chip = lax.rem(me, 2), me // 2
     hid_rows, width = hid_ref.shape
     tile, up_tile = wide.shape[2], up.shape[2]
-    wide_slots, up_slots = wide.shape[0], up.shape[0]
+    up_slots = up.shape[0]
     n_wide, n_up = width // tile, wu_ref.shape[2] // up_tile
 
     def peer(j):
@@ -709,9 +706,6 @@
         return carry
 
     lax.fori_loop(0, n_wide, add_out, 0)
-    if follow:
-        for t in range(wide_slots):
-            wide_copy(proj[t // n_wide], layer + 1, t % n_wide, t).start()
     acc_scr[...] = jnp.zeros_like(acc_scr)
 
     def mlp(t, carry):
@@ -731,32 +725,14 @@
     lax.fori_loop(0, n_up, mlp, 0)
     hid_out[...] = (mid_scr[...].astype(jnp.float32) + acc_scr[...]).astype(jnp.bfloat16)
 
-    if follow:
-        xs, all_held, pass_send, pass_recv, spread_send, spread_recv, copy_sem = refs
-        other = me + 1 - 2 * core
-        for m in range(3):
-            def project(t, carry):
-                slot = lax.rem(m * n_wide + t, wide_slots)
-                wide_copy(proj[m], layer + 1, t, slot).wait()
-                part = jnp.dot(hid_out[...], wide[slot], preferred_element_type=jnp.float32)
-                acc_scr[:, pl.ds(pl.multiple_of(t * tile, tile), tile)] = part
-                if m < 2:
-                    wide_copy(proj[m + 1], layer + 1, t, slot).start()
-                return carry
-
-            lax.fori_loop(0, n_wide, project, 0)
-            for h in range(heads):
-                o_scr[pl.ds(h, hid_rows, stride=heads), :] = acc_scr[:, h * head_dim:(h + 1) * head_dim]
-            for i in range(seq_dev):
-                xs[m, i] = o_scr[i * rows:(i + 1) * rows].astype(jnp.bfloat16)
-        x_out[...] = xs[...]
-        spread_body(n, xs, all_out, all_held, spread_send, spread_recv, pass_send, pass_recv, copy_sem)
-
     def finish(j, carry):
         send(j).wait_send()
         return carry
 
     lax.fori_loop(1, chips, finish, 0)
+    if follow:
+        all_held, pass_send, pass_recv, spread_send, spread_recv, copy_sem = refs
+        spread_body(n, hid_out, all_out, all_held, spread_send, spread_recv, pass_send, pass_recv, copy_sem)
 
     def pages_came(j, carry):
         at = lax.rem(me + n - j, n)
@@ -770,11 +746,10 @@
     lax.fori_loop(1, n, pages_came, 0)
 
 
-def end_layer(sums, x, hidden, chunk, w_out, w_up, w_down, proj, layer, n):
+def end_layer(sums, x, hidden, chunk, w_out, w_up, w_down, layer, follow, n):
     chips = n // 2
     hid_rows, width = hidden.shape
     seq_dev, rows, head_dim = x.shape[1:]
-    follow = bool(proj)
     tile, up_slots = 512, 3
     wide_slots = width // tile
     out_shape = [jax.ShapeDtypeStruct(hidden.shape, hidden.dtype), jax.ShapeDtypeStruct(chunk.shape, chunk.dtype)]
@@ -797,21 +772,21 @@
         pltpu.SemaphoreType.DMA((n,)),
     ]
     if follow:
-        spread_shape = (2, chips) + x.shape
-        out_shape += [jax.ShapeDtypeStruct(x.shape, x.dtype), jax.ShapeDtypeStruct(spread_shape, x.dtype)]
-        out_specs += [VMEM, ANY]
-        scratch += [pltpu.VMEM(x.shape, x.dtype), pltpu.VMEM(spread_shape, x.dtype)]
+        spread_shape = (2, chips) + hidden.shape
+        out_shape += [jax.ShapeDtypeStruct(spread_shape, hidden.dtype)]
+        out_specs += [ANY]
+        scratch += [pltpu.VMEM(spread_shape, hidden.dtype)]
         scratch += [pltpu.SemaphoreType.DMA((chips,))] * 4 + [pltpu.SemaphoreType.DMA((n,))]
     return pl.pallas_call(
         functools.partial(layer_kernel, n, head_dim ** -0.5, layer, follow),
         out_shape=out_shape,
-        in_specs=[VMEM] * 3 + [ANY] * (4 + len(proj)),
+        in_specs=[VMEM] * 3 + [ANY] * 4,
         out_specs=out_specs,
         scratch_shapes=scratch,
         compiler_params=pltpu.CompilerParams(collective_id=3 + layer, has_side_effects=True),
         cost_estimate=pl.CostEstimate(flops=10 ** 10, bytes_accessed=2 ** 27, transcendentals=0),
         name="end_layer",
-    )(sums, x, hidden, chunk, w_out, w_up, w_down, *proj)
+    )(sums, x, hidden, chunk, w_out, w_up, w_down)
 
 
 def solution(mesh):
@@ -868,35 +843,39 @@
                 got.append(exchange(block))
             return value
 
-        plan = ((0, (0,)), (0, (1,))) + tuple((r, (0, 1)) for r in range(1, rounds - 1)) + ((rounds - 1, (0,)), (rounds - 1, (1,)))
+        plan = tuple((r, (0, 1)) for r in range(rounds - 1)) + ((rounds - 1, (0,)), (rounds - 1, (1,)))
         packed = list(pack_pages(plan[:1], send_slot, k_pool, v_pool, groups))
         packed[0], send_slot = lax.optimization_barrier((packed[0], send_slot))
-        got = [exchange(packed[0])]
         packed += list(pack_pages(plan[1:], send_slot, k_pool, v_pool, groups))
+        got = []
         tables = (from_page, first_seq, second_seq, offsets)
         k_out, v_out = keep_pages(from_page, k_pool, v_pool)
 
         hidden = jnp.transpose(embeds, (1, 0, 2)).reshape(seq_dev * steps, width)
-        x = jnp.stack([
-            jnp.dot(hidden, w[0], preferred_element_type=jnp.float32).astype(jnp.bfloat16).reshape(seq_dev, steps * heads, head_dim)
-            for w in (w_query, w_key, w_value)
-        ])
-        x, k_out, v_out, packed, got = lax.optimization_barrier((x, k_out, v_out, packed, got))
-        x_all = spread(x, groups)
+        every = spread(hidden, groups)
         rows = []
         for layer in range(n_layers):
-            rows.append(x_all)
-            x_all = send_next(x_all, 1)
-            sums = merge_chip(attend_pages(code, x_all, k_pool, v_pool, layer, pages_seq))
+            every, got = lax.optimization_barrier((every, got))
+            every = send_next(every, 1)
+            flat_rows = every.reshape(groups * seq_dev * steps, width)
+            every_x = [
+                jnp.dot(flat_rows, w[layer], preferred_element_type=jnp.float32).astype(jnp.bfloat16)
+                .reshape(2, groups // 2, seq_dev, steps * heads, head_dim)
+                for w in (w_query, w_key, w_value)
+            ]
+            rows += every_x[1:]
+            x = jnp.stack([y[lax.rem(me, 2), me // 2] for y in every_x])
+            sums = merge_chip(attend_pages(code, every_x[0], k_pool, v_pool, layer, pages_seq))
             if layer:
-                k_out, v_out = place_pages(plan[:3], from_page, got[:3], k_out, v_out)
-                sums, k_out, v_out = lax.optimization_barrier((sums, k_out, v_out))
-            follow = (w_query, w_key, w_value) if layer + 1 < n_layers else ()
-            hidden, pages, *ahead = end_layer(sums, x, hidden, packed[len(got)], w_out, w_up, w_down, follow, layer, groups)
+                k_out, v_out = place_pages(plan[:2], from_page, got[:2], k_out, v_out)
+            sums, k_out, v_out, packed = lax.optimization_barrier((sums, k_out, v_out, packed))
+            hidden, pages, *ahead = end_layer(
+                sums, x, hidden, packed[len(got)], w_out, w_up, w_down, layer, layer + 1 < n_layers, groups
+            )
             got.append(pages)
             if ahead:
-                x, x_all = ahead
-        k_out, v_out = close_pools(seq_dev, rounds - 1, *tables, got[3:], rows, k_out, v_out)
+                (every,) = ahead
+        k_out, v_out = close_pools(seq_dev, rounds - 1, *tables, got[2:], rows, k_out, v_out)
         hidden = jnp.transpose(hidden.reshape(seq_dev, steps, width), (1, 0, 2))
         done = lax.dynamic_slice(finished, (me * seq_dev,), (seq_dev,)) != 0
         live = jnp.stack([jnp.ones_like(done), ~done])

time: 461 us -> 439 us (0.952)
  Pallas kernels: 390 us -> 361 us
  waiting for transfers between devices: 25.2 us -> 0.01 us
  matrix products: 13.7 us -> 38.4 us
  local copies, waits for them, and re-layouts: 1.28 us -> 10.9 us
    pallas_call x2, Pallas kernels: 277 us -> 250 us  [end_layer(): pl.pallas_call(functools.partial(layer_kernel, n, head_dim ** (-0.5), lay...]
    all_to_all x3 -> x2, waiting for transfers between devices: 25.2 us -> 0.01 us  [exchange(): return lax.all_to_all(block, 'kv', 0, 0, tiled=True)]
    dot_general x3 -> x6, matrix products: 13.7 us -> 38.4 us  [device_fn(): jnp.dot(flat_rows, w[layer], preferred_element_type=jnp.float32)]
    pallas_call x2, Pallas kernels: 6.65 us -> 17.5 us  [pack_pages(): pl.pallas_call(functools.partial(pack_kernel, depth, lead, plan), out_sha...]
    pallas_call x1, Pallas kernels: 31.6 us -> 21.7 us  [spread(): pl.pallas_call(functools.partial(spread_kernel, n), out_shape=jax.ShapeDt...]
    pallas_call x1, Pallas kernels: 12.5 us -> 4.19 us  [place_pages(): pl.pallas_call(functools.partial(place_kernel, depth, lead, plan), out_sh...]
    pallas_call x1, Pallas kernels: 7.34 us -> 15.5 us  [keep_pages(): pl.pallas_call(functools.partial(keep_kernel, depth, lead), out_shape=[ja...]
    reshape x0 -> x6, local copies, waits for them, and re-layouts: none -> 6.76 us  [device_fn(): every_x = [jnp.dot(flat_rows, w[layer], preferred_element_type=jnp.float3...]
  transfers between devices with their start and end apart: 3 -> 2, of which waited for: 1 -> 0; matrix products, arithmetic and copies ran while one was open for 4% -> 12% of each run, Pallas kernels for 75% -> 75%
where the time goes in v3:
time: 439 us; the launch traced here: 438 us
  Pallas kernels  361 us (82%)
  matrix products  38.4 us (9%)
  starting transfers between devices  17.4 us (4%)
  local copies, waits for them, and re-layouts  10.9 us (2%)
  other arithmetic  8.69 us (2%)
    pallas_call x2, Pallas kernels, end_layer(): pl.pallas_call(functools.partial(layer_kernel, n, head_dim ** (-0.5), lay...  250 us
    dot_general x6, matrix products, device_fn(): jnp.dot(flat_rows, w[layer], preferred_element_type=jnp.float32)  38.4 us
    pallas_call x2, Pallas kernels, attend_pages(): pl.pallas_call(functools.partial(attend_kernel, block, pages_seq, seq_dev...  28.1 us
    pallas_call x1, Pallas kernels, spread(): pl.pallas_call(functools.partial(spread_kernel, n), out_shape=jax.ShapeDt...  21.7 us
    pallas_call x2, Pallas kernels, pack_pages(): pl.pallas_call(functools.partial(pack_kernel, depth, lead, plan), out_sha...  17.5 us
    all_to_all x2, starting transfers between devices, exchange(): return lax.all_to_all(block, 'kv', 0, 0, tiled=True)  17.4 us
    pallas_call x2, Pallas kernels, merge_chip(): pl.pallas_call(merge_chip_kernel, out_shape=jax.ShapeDtypeStruct(blocks,...  16.8 us
    pallas_call x1, Pallas kernels, keep_pages(): pl.pallas_call(functools.partial(keep_kernel, depth, lead), out_shape=[ja...  15.5 us
  transfers between devices with their start and end apart: 2, of which 0 were waited for; matrix products, arithmetic and copies ran while one was open for 12% of the time, Pallas kernels for 75%

profile of v3, /device:TPU:97, one launch (start us, length us, event | category | flops | bytes accessed | tf_op | source)
XLA Modules:
  0.0 437.6 jit_solution(17950414161305000412)
XLA Ops:
  0.6 0.7 broadcast_compare_fusion
  1.3 0.7 multiply_add_fusion.1
  2.1 0.4 convert_reduce_fusion
  2.4 0.8 copy.33
  3.2 0.6 reshape.102.x_ref.refs_2_
  3.9 21.7 %spread_rows.1 = bf16[2,16,8,2048]{3,2,1,0:T(8,128)(2,1)} custom-call(bf16[8,2048]{1,0:T(8,128)(2,1)} %reshape.102.x_ref.refs_2_), custom_call_target="tpu_custom_call" | custom-call | tf_op jit(solution)/shard_map/spread_rows/pallas_call | solution.py:504
  25.6 0.7 broadcast_subtract_fusion.1
  26.3 0.7 select_reduce_fusion.1.slot_ref
  27.0 5.9 %pack_pages.2 = bf16[32,2,2,16,16,128]{5,4,3,2,1,0:T(8,128)(2,1)} custom-call(s32[96]{0:T(128)} %select_reduce_fusion.1.slot_ref, bf16[72,2,16,16,128]{4,3,2,1,0:T(8,128)(2,1)} %k_ref.5, bf16[72,2,16,16,128]{4,3,2,1,0:T(8,128)(2,1)} %v_ref.5), custom_call_target="tpu_custom_call" | custom-call | flops 1000000 | bytes 4194304 | tf_op jit(solution)/shard_map/pack_pages/pallas_call | solution.py:114
  32.9 4.0 all-to-all-start
  37.0 0.1 copy.32
  37.1 0.1 sub.87
  37.3 0.1 min.12
  37.4 5.7 %fusion.24 = bf16[256,2048]{1,0:T(8,128)(2,1)S(1)} fusion(bf16[256,2048]{1,0:T(8,128)(2,1)S(1)} %bitcast.62, bf16[2,2048,2048]{2,1,0:T(8,128)(2,1)} %param.18), kind=kOutput, calls=%fused_computation.20 | convolution fusion | flops 2148007936 | bytes 10485760 | tf_op jit(solution)/shard_map/dot_general | solution.py:862
  43.1 0.5 reshape.106.rest_1_
  43.7 7.1 %fusion.21 = bf16[256,2048]{1,0:T(8,128)(2,1)} fusion(bf16[256,2048]{1,0:T(8,128)(2,1)S(1)} %bitcast.63, bf16[2,2048,2048]{2,1,0:T(8,128)(2,1)} %param.17), kind=kOutput, calls=%fused_computation.19 | convolution fusion | flops 2148007936 | bytes 10485760 | tf_op jit(solution)/shard_map/dot_general | solution.py:862
  50.7 1.6 reshape.105.rest_0_
  52.3 7.1 %fusion.18 = bf16[256,2048]{1,0:T(8,128)(2,1)} fusion(bf16[256,2048]{1,0:T(8,128)(2,1)S(1)} %bitcast.64, bf16[2,2048,2048]{2,1,0:T(8,128)(2,1)} %param.16), kind=kOutput, calls=%fused_computation.18 | convolution fusion | flops 2148007936 | bytes 10485760 | tf_op jit(solution)/shard_map/dot_general | solution.py:862
  59.4 2.3 reshape.104.q_ref
  61.7 0.8 select_reduce_fusion.code_ref
  62.5 14.1 %attend_pages.2.acc_ref = f32[2,16,5,32,128]{4,3,2,1,0:T(8,128)} custom-call(s32[72]{0:T(128)} %select_reduce_fusion.code_ref, bf16[2,16,4,32,128]{4,3,2,1,0:T(8,128)(2,1)} %reshape.104.q_ref, bf16[72,2,16,16,128]{4,3,2,1,0:T(8,128)(2,1)} %k_ref.5, bf16[72,2,16,16,128]{4,3,2,1,0:T(8,128)(2,1)} %v_ref.5), custom_call_target="tpu_custom_call" | custom-call | flops 1000000 | bytes 9437184 | tf_op jit(solution)/shard_map/attend_pages/pallas_call | solution.py:401
  76.5 8.3 %merge_chip.2.refs_0_ = f32[16,5,32,128]{3,2,1,0:T(8,128)} custom-call(f32[2,16,5,32,128]{4,3,2,1,0:T(8,128)} %attend_pages.2.acc_ref), custom_call_target="tpu_custom_call" | custom-call | flops 1000000 | bytes 8388608 | tf_op jit(solution)/shard_map/merge_chip/pallas_call | solution.py:561
  84.8 11.7 %pack_pages.3 = (bf16[32,2,2,16,16,128]{5,4,3,2,1,0:T(8,128)(2,1)}, bf16[32,1,2,16,16,128]{5,4,3,2,1,0:T(8,128)(2,1)}, bf16[32,1,2,16,16,128]{5,4,3,2,1,0:T(8,128)(2,1)}) custom-call(s32[96]{0:T(128)} %select_reduce_fusion.1.slot_ref, bf16[72,2,16,16,128]{4,3,2,1,0:T(8,128)(2,1)} %k_ref.5, bf16[72,2,16,16,128]{4,3,2,1,0:T(8,128)(2,1)} %v_ref.5), custom_call_target="tpu_custom_call" | custom-call | flops 1000000 | bytes 8388608 | tf_op jit(solution)/shard_map/pack_pages/pallas_call | solution.py:114
  96.5 0.6 select_reduce_fusion.2.from_ref
  97.1 15.5 %keep_pages.1 = (bf16[72,2,16,16,128]{4,3,2,1,0:T(8,128)(2,1)}, bf16[72,2,16,16,128]{4,3,2,1,0:T(8,128)(2,1)}) custom-call(s32[72]{0:T(128)} %select_reduce_fusion.2.from_ref, bf16[72,2,16,16,128]{4,3,2,1,0:T(8,128)(2,1)} %k_ref.5, bf16[72,2,16,16,128]{4,3,2,1,0:T(8,128)(2,1)} %v_ref.5), custom_call_target="tpu_custom_call" | custom-call | flops 1000000 | bytes 33554432 | tf_op jit(solution)/shard_map/keep_pages/pallas_call | solution.py:152
  112.6 0.8 dynamic-slice_bitcast_fusion.5
  113.4 0.7 subtract_bitcast_fusion.1
  114.1 0.1 select_reduce_fusion.3
  114.3 0.7 pad_maximum_fusion.refs_1_
  114.9 0.5 compare_select_fusion.offset_ref
  115.4 0.6 compare_select_fusion.2.first_ref
  116.0 168.9 %end_layer.2 = (bf16[8,2048]{1,0:T(8,128)(2,1)}, bf16[32,2,2,16,16,128]{5,4,3,2,1,0:T(8,128)(2,1)}, bf16[2,16,8,2048]{3,2,1,0:T(8,128)(2,1)}) custom-call(f32[16,5,32,128]{3,2,1,0:T(8,128)} %merge_chip.2.refs_0_, bf16[3,4,32,128]{3,2,1,0:T(8,128)(2,1)} %pad_maximum_fusion.refs_1_, bf16[8,2048]{1,0:T(8,128)(2,1)} %reshape.102.x_ref.refs_2_, ...), custom_call_target="tpu_custom_call" | custom-call | flops 10000000000 | bytes 134217728 | tf_op jit(solution)/shard_map/end_layer/pallas_call | solution.py:780
  284.9 13.4 %all-to-all-start.1 = ((bf16[32,1,2,16,16,128]{5,4,3,2,1,0:T(8,128)(2,1)}), bf16[32,1,2,16,16,128]{5,4,3,2,1,0:T(8,128)(2,1)}, u32[]{:S(2)}, u32[]{:S(2)}) async-start(bf16[32,1,2,16,16,128]{5,4,3,2,1,0:T(8,128)(2,1)} %get-tuple-element.63), calls=%async_computation.1 | async-start | bytes 8388608 | tf_op jit(solution)/shard_map/all_to_all | solution.py:838
  298.4 5.7 %fusion.33 = bf16[256,2048]{1,0:T(8,128)(2,1)S(1)} fusion(bf16[256,2048]{1,0:T(8,128)(2,1)S(1)} %bitcast.68, bf16[2,2048,2048]{2,1,0:T(8,128)(2,1)} %param.18), kind=kOutput, calls=%fused_computation.23 | convolution fusion | flops 2148007936 | bytes 10485760 | tf_op jit(solution)/shard_map/dot_general | solution.py:862
  304.2 0.5 reshape.110.rest_3_
  304.7 6.4 %fusion.30 = bf16[256,2048]{1,0:T(8,128)(2,1)S(1)} fusion(bf16[256,2048]{1,0:T(8,128)(2,1)} %bitcast.66, bf16[2,2048,2048]{2,1,0:T(8,128)(2,1)} %param.17), kind=kOutput, calls=%fused_computation.22 | convolution fusion | flops 2148007936 | bytes 10485760 | tf_op jit(solution)/shard_map/dot_general | solution.py:862
  311.1 0.5 reshape.109.rest_2_
  311.7 6.4 %fusion.27 = bf16[256,2048]{1,0:T(8,128)(2,1)S(1)} fusion(bf16[256,2048]{1,0:T(8,128)(2,1)} %bitcast.67, bf16[2,2048,2048]{2,1,0:T(8,128)(2,1)} %param.16), kind=kOutput, calls=%fused_computation.21 | convolution fusion | flops 2148007936 | bytes 10485760 | tf_op jit(solution)/shard_map/dot_general | solution.py:862
  318.1 1.3 reshape.108.q_ref
  319.4 14.1 %attend_pages.3.acc_ref = f32[2,16,5,32,128]{4,3,2,1,0:T(8,128)} custom-call(s32[72]{0:T(128)} %select_reduce_fusion.code_ref, bf16[2,16,4,32,128]{4,3,2,1,0:T(8,128)(2,1)} %reshape.108.q_ref, bf16[72,2,16,16,128]{4,3,2,1,0:T(8,128)(2,1)} %k_ref.5, bf16[72,2,16,16,128]{4,3,2,1,0:T(8,128)(2,1)} %v_ref.5), custom_call_target="tpu_custom_call" | custom-call | flops 1000000 | bytes 9437184 | tf_op jit(solution)/shard_map/attend_pages/pallas_call | solution.py:401
  333.4 8.5 %merge_chip.3.refs_0_ = f32[16,5,32,128]{3,2,1,0:T(8,128)} custom-call(f32[2,16,5,32,128]{4,3,2,1,0:T(8,128)} %attend_pages.3.acc_ref), custom_call_target="tpu_custom_call" | custom-call | flops 1000000 | bytes 8388608 | tf_op jit(solution)/shard_map/merge_chip/pallas_call | solution.py:561
  342.0 4.2 place_pages.1
  346.2 0.8 dynamic-slice_bitcast_fusion.2
  346.9 0.7 pad_maximum_fusion.1.refs_1_
  347.6 81.3 %end_layer.3 = (bf16[8,2048]{1,0:T(8,128)(2,1)}, bf16[32,1,2,16,16,128]{5,4,3,2,1,0:T(8,128)(2,1)}) custom-call(f32[16,5,32,128]{3,2,1,0:T(8,128)} %merge_chip.3.refs_0_, bf16[3,4,32,128]{3,2,1,0:T(8,128)(2,1)} %pad_maximum_fusion.1.refs_1_, bf16[8,2048]{1,0:T(8,128)(2,1)} %get-tuple-element.60.refs_2_, ...), custom_call_target="tpu_custom_call" | custom-call | flops 10000000000 | bytes 134217728 | tf_op jit(solution)/shard_map/end_layer/pallas_call | solution.py:780
  428.9 0.8 reshape.111
  429.7 0.7 bitcast_select_fusion
  430.4 7.0 %close_pools.1 = (bf16[72,2,16,16,128]{4,3,2,1,0:T(8,128)(2,1)}, bf16[72,2,16,16,128]{4,3,2,1,0:T(8,128)(2,1)}) custom-call(s32[72]{0:T(128)} %select_reduce_fusion.2.from_ref, s32[72]{0:T(128)} %compare_select_fusion.2.first_ref, s32[72]{0:T(128)} %copy-done.7, s32[128]{0:T(128)} %compare_select_fusion.offset_ref, ...), custom_call_target="tpu_custom_call", output_to_operand_aliasing={{0}: (10, {}), {1}: (11, {})} | custom-call | flops 1000000 | bytes 8388608 | tf_op jit(solution)/shard_map/close_pools/pallas_call | solution.py:323
  (35 shorter events, 0.3 us)
Async XLA Ops:
  32.8 4.1 copy-start.6
  32.9 4.3 copy-start.8
  32.9 4.5 %copy-start.4 = (bf16[2,16,8,2048]{3,2,1,0:T(8,128)(2,1)S(1)}, bf16[2,16,8,2048]{3,2,1,0:T(8,128)(2,1)}, u32[]{:S(2)}) copy-start(bf16[2,16,8,2048]{3,2,1,0:T(8,128)(2,1)} %spread_rows.1) | copy-start | bytes 3145732
  32.9 252.0 %all-to-all-start = ((bf16[32,2,2,16,16,128]{5,4,3,2,1,0:T(8,128)(2,1)}), bf16[32,2,2,16,16,128]{5,4,3,2,1,0:T(8,128)(2,1)}, u32[]{:S(2)}, u32[]{:S(2)}) async-start(bf16[32,2,2,16,16,128]{5,4,3,2,1,0:T(8,128)(2,1)} %pack_pages.2), calls=%async_computation | async-start | bytes 16777216 | tf_op jit(solution)/shard_map/all_to_all | solution.py:838
  43.7 69.7 %copy-start = (bf16[2,16,4,32,128]{4,3,2,1,0:T(8,128)(2,1)}, bf16[2,16,4,32,128]{4,3,2,1,0:T(8,128)(2,1)S(1)}, u32[]{:S(2)}) copy-start(bf16[2,16,4,32,128]{4,3,2,1,0:T(8,128)(2,1)S(1)} %reshape.106.rest_1_) | copy-start | bytes 3145732
  52.3 61.1 %copy-start.1 = (bf16[2,16,4,32,128]{4,3,2,1,0:T(8,128)(2,1)}, bf16[2,16,4,32,128]{4,3,2,1,0:T(8,128)(2,1)S(1)}, u32[]{:S(2)}) copy-start(bf16[2,16,4,32,128]{4,3,2,1,0:T(8,128)(2,1)S(1)} %reshape.105.rest_0_) | copy-start | bytes 3145732
  97.1 16.3 %copy-start.10 = (s32[128]{0:T(128)S(1)}, s32[128]{0:T(128)}, u32[]{:S(2)}) copy-start(s32[128]{0:T(128)} %param.27) | copy-start | bytes 1540
  97.1 18.4 %copy-start.5 = (s32[72]{0:T(128)S(1)}, s32[72]{0:T(128)}, u32[]{:S(2)}) copy-start(s32[72]{0:T(128)} %select_reduce_fusion.2.from_ref) | copy-start | bytes 868
  114.2 170.7 %copy-start.7 = (s32[72]{0:T(128)}, s32[72]{0:T(128)S(1)}, u32[]{:S(2)}) copy-start(s32[72]{0:T(128)S(1)} %get-tuple-element.76.second_ref) | copy-start | bytes 868
  284.9 13.5 %copy-start.9 = (bf16[2,16,8,2048]{3,2,1,0:T(8,128)(2,1)S(1)}, bf16[2,16,8,2048]{3,2,1,0:T(8,128)(2,1)}, u32[]{:S(2)}) copy-start(bf16[2,16,8,2048]{3,2,1,0:T(8,128)(2,1)} %get-tuple-element.51) | copy-start | bytes 3145732
  284.9 145.4 %all-to-all-start.1 = ((bf16[32,1,2,16,16,128]{5,4,3,2,1,0:T(8,128)(2,1)}), bf16[32,1,2,16,16,128]{5,4,3,2,1,0:T(8,128)(2,1)}, u32[]{:S(2)}, u32[]{:S(2)}) async-start(bf16[32,1,2,16,16,128]{5,4,3,2,1,0:T(8,128)(2,1)} %get-tuple-element.63), calls=%async_computation.1 | async-start | bytes 8388608 | tf_op jit(solution)/shard_map/all_to_all | solution.py:838
  304.7 42.2 %copy-start.2 = (bf16[2,16,4,32,128]{4,3,2,1,0:T(8,128)(2,1)}, bf16[2,16,4,32,128]{4,3,2,1,0:T(8,128)(2,1)S(1)}, u32[]{:S(2)}) copy-start(bf16[2,16,4,32,128]{4,3,2,1,0:T(8,128)(2,1)S(1)} %reshape.110.rest_3_) | copy-start | bytes 3145732
  311.6 35.3 %copy-start.3 = (bf16[2,16,4,32,128]{4,3,2,1,0:T(8,128)(2,1)}, bf16[2,16,4,32,128]{4,3,2,1,0:T(8,128)(2,1)S(1)}, u32[]{:S(2)}) copy-start(bf16[2,16,4,32,128]{4,3,2,1,0:T(8,128)(2,1)S(1)} %reshape.109.rest_2_) | copy-start | bytes 3145732
